TPU v7x, 128 devices: a whole 4x4x4 slice. The times are simulated.
128 devices in a mesh: seq: 16 (over z, x), exp: 8 (over y, core).
Axes of the slice: x: 4, y: 4, z: 4, core: 2. Of those that a mesh axis runs over, the one named last changes fastest.
Arguments:
- tokens: bfloat16 [8, 2048, 4096], P('exp', 'seq'), may hold values from -6 to 6
- out_grad: bfloat16 [8, 2048, 4096], P('exp', 'seq'), may hold values from -0.59765625 to 0.59765625
- router_weight: bfloat16 [4096, 128], replicated, may hold values from -8 to 8
- gate_weight: bfloat16 [128, 4096, 768], P(('seq', 'exp')), may hold values from -0.09375 to 0.09375
- up_weight: bfloat16 [128, 4096, 768], P(('seq', 'exp')), may hold values from -0.09375 to 0.09375
- down_weight: bfloat16 [128, 768, 4096], P(('seq', 'exp')), may hold values from -0.21875 to 0.21875
- saved_gate: bfloat16 [128, 2048, 768], P(('seq', 'exp')), may hold values from -6 to 6
- saved_up: bfloat16 [128, 2048, 768], P(('seq', 'exp')), may hold values from -6 to 6
- expert_ids: int32 [8, 2048, 8], P('exp', 'seq'), may hold values from 0 to 127, as said below
- aux_weight: float32 [1], replicated, may hold values from 2 to 6
Outputs:
- token_grad: bfloat16 [8, 2048, 4096], P('exp', 'seq')
- combine_grad: float32 [8, 2048, 8], P('exp', 'seq')
- router_grad: float32 [4096, 128], P(('seq', 'exp'))
Inputs may be any that keep to these rules, and one draw needn't show every extreme that they name: `expert_ids`: among the rows of one device (128 tokens) each expert is named at most 16 times, and some expert exactly 16 times; a token's 8 experts differ.
All inputs are finite; a program needn't handle non-finite values.
Results may differ from a plain program's by a relative error of at most 0.013.
Values may be sent and summed in bfloat16 or wider, within the bound.
A program may use at most 192 MiB of HBM per device.

v0:
```python
import functools

import jax
import jax.numpy as jnp
from jax import lax
from jax.experimental import pallas as pl
from jax.experimental.pallas import tpu as pltpu
from jax.sharding import Mesh
from jax.sharding import PartitionSpec as P

SEQ = ("seq_0", "seq_1")
EXP = ("exp_0", "exp_1")
AXES = ("seq_0", "seq_1", "exp_0", "exp_1")
MESH = pl.DeviceIdType.MESH
RING = 4
LANES = 128
ORDERS = ((0, 1, 2), (1, 2, 0), (2, 0, 1))


def column_parts(width):
    tiles = width // LANES
    sizes = [(tiles + 2 - p) // 3 * LANES for p in range(3)]
    starts = [0, sizes[0], sizes[0] + sizes[1]]
    return list(zip(starts, sizes))


class Wires:
    def __init__(self, send_sems, recv_sems):
        self.send_sems, self.recv_sems = send_sems, recv_sems
        self.sent, self.names = [], {}

    def slot(self, name):
        return self.recv_sems.at[self.names.setdefault(name, len(self.names))]

    def send(self, src, dst, device, name):
        copy = pltpu.make_async_remote_copy(
            src, dst, self.send_sems.at[len(self.sent)], self.slot(name), device, MESH
        )
        copy.start()
        self.sent.append(copy)

    def arrived(self, ref, name, device):
        pltpu.make_async_remote_copy(
            ref, ref, self.send_sems.at[0], self.slot(name), device, MESH
        ).wait_recv()

    def drain(self):
        for copy in self.sent:
            copy.wait_send()


class Place:
    def __init__(self):
        self.at = [lax.axis_index(name) for name in AXES]
        self.core = self.at[3]

    def along(self, axis, step):
        return lax.rem(self.at[axis] + (step + RING), RING)

    def near(self, axis, step, other_core=0):
        coords = list(self.at)
        coords[axis] = self.along(axis, step)
        if other_core:
            coords[3] = 1 - self.core
        return tuple(coords)

    def partner(self):
        return (self.at[0], self.at[1], self.at[2], 1 - self.core)

    def greet(self):
        barrier = pltpu.get_barrier_semaphore()
        peers = [self.partner()]
        for axis in range(3):
            for step in (1, -1):
                for other in (0, 1):
                    peers.append(self.near(axis, step, other))
        for peer in peers:
            pl.semaphore_signal(barrier, inc=1, device_id=peer, device_id_type=MESH)
        pl.semaphore_wait(barrier, len(peers))


def slots_of(ref, order, b_index, s_index, c_index, start, size):
    a, b, s = order
    where = [None] * 3
    where[a], where[b], where[s] = slice(None), b_index, s_index
    return ref.at[where[0], where[1], where[2], c_index, :, pl.ds(start, size)]


def line_row(table, line):
    rows = table.astype(jnp.float32)
    index = lax.broadcasted_iota(jnp.int32, rows.shape, 0)
    return jnp.sum(jnp.where(index == line, rows, 0.0), axis=0, keepdims=True)


def fixed_b(order, b_index):
    where = [slice(None)] * 3
    where[order[1]] = b_index
    return tuple(where)


def dispatch_kernel(
    parts, grad, maps, down, slots, maps_out, upstream,
    g0, g1, g2, o0, o1, o2, l0, l1, l2, seen, weight, batch, ss, rs, ls, bs,
):
    held, outgoing, relay = (g0, g1, g2), (o0, o1, o2), (l0, l1, l2)
    here = Place()
    wires = Wires(ss, rs)
    tokens = grad.shape[0]
    half = tokens // 2
    local = []

    def keep(src, dst):
        copy = pltpu.make_async_copy(src, dst, ls.at[len(local)])
        copy.start()
        local.append(copy)

    for p, (a, b, s) in enumerate(ORDERS):
        start, size = parts[p]
        keep(grad.at[:, pl.ds(start, size)], held[p].at[here.at[b], here.at[a]])
        keep(maps.at[p], seen.at[p, here.at[b], here.at[a]])
    fetch = pltpu.make_async_copy(down, weight, bs.at[2])
    fetch.start()
    here.greet()
    for copy in local:
        copy.wait()

    def pass_on(p, k, step):
        a, b, s = ORDERS[p]
        block = held[p].at[here.at[b], here.along(a, step)]
        wires.send(block, block, here.near(b, 1), (p, "m2", 1, k))
        wires.send(block, block, here.near(b, -1), (p, "m2", -1, k))

    def relay_on(p, k, step):
        a, b, s = ORDERS[p]
        for way, rows in ((1, pl.ds(0, half)), (-1, pl.ds(half, half))):
            block = held[p].at[here.along(b, -way), here.along(a, step)]
            wires.arrived(block, (p, "m2", way, k), here.near(b, -way))
            piece = held[p].at[here.along(b, -way), here.along(a, step), rows]
            wires.send(piece, piece, here.near(b, way), (p, "m2far", way, k))

    def far_in(p, k, step):
        a, b, s = ORDERS[p]
        for way, rows in ((1, pl.ds(0, half)), (-1, pl.ds(half, half))):
            piece = held[p].at[here.along(b, 2), here.along(a, step), rows]
            wires.arrived(piece, (p, "m2far", way, k), here.near(b, -way))

    for p, (a, b, s) in enumerate(ORDERS):
        table = seen.at[p, here.at[b], here.at[a]]
        block = held[p].at[here.at[b], here.at[a]]
        for way in (1, -1):
            wires.send(table, table, here.near(a, way), (p, "t1", way))
        for way in (1, -1):
            wires.send(block, block, here.near(a, way), (p, "m1", way))
    for p in range(3):
        pass_on(p, 0, 0)
    for p, (a, b, s) in enumerate(ORDERS):
        table = seen.at[p, here.at[b], here.along(a, -1)]
        wires.arrived(table, (p, "t1", 1), here.near(a, -1))
        wires.send(table, table, here.near(a, 1), (p, "t1far"))
        wires.arrived(
            seen.at[p, here.at[b], here.along(a, 1)], (p, "t1", -1), here.near(a, 1)
        )
    for p, (a, b, s) in enumerate(ORDERS):
        for way, rows in ((1, pl.ds(0, half)), (-1, pl.ds(half, half))):
            block = held[p].at[here.at[b], here.along(a, -way)]
            wires.arrived(block, (p, "m1", way), here.near(a, -way))
            piece = held[p].at[here.at[b], here.along(a, -way), rows]
            wires.send(piece, piece, here.near(a, way), (p, "m1far", way))
    for p, (a, b, s) in enumerate(ORDERS):
        wires.arrived(
            seen.at[p, here.at[b], here.along(a, 2)], (p, "t1far"), here.near(a, -1)
        )
        table = seen.at[p, here.at[b]]
        for way in (1, -1):
            wires.send(table, table, here.near(b, way), (p, "t2", way))
    for p in range(3):
        pass_on(p, 1, -1)
        pass_on(p, 2, 1)
    for p, (a, b, s) in enumerate(ORDERS):
        table = seen.at[p, here.along(b, -1)]
        wires.arrived(table, (p, "t2", 1), here.near(b, -1))
        wires.send(table, table, here.near(b, 1), (p, "t2far"))
        wires.arrived(seen.at[p, here.along(b, 1)], (p, "t2", -1), here.near(b, 1))
    for p, (a, b, s) in enumerate(ORDERS):
        for way, rows in ((1, pl.ds(0, half)), (-1, pl.ds(half, half))):
            piece = held[p].at[here.at[b], here.along(a, 2), rows]
            wires.arrived(piece, (p, "m1far", way), here.near(a, -way))
        pass_on(p, 3, 2)

    def select(p, k, b_step):
        a, b, s = ORDERS[p]
        b_index = here.along(b, b_step)
        line = here.at[b] * RING + here.at[a]
        size = parts[p][1]

        def one(a_index, carry):
            token_of = line_row(seen[p, b_index, a_index, pl.ds(0, 16), :], line)
            token = lax.broadcasted_iota(jnp.int32, (tokens, LANES), 0).astype(jnp.float32)
            pick = jnp.where(token == token_of, 1.0, 0.0).astype(jnp.bfloat16)
            rows = lax.dot_general(
                pick,
                held[p][b_index, a_index],
                (((0,), (0,)), ((), ())),
                preferred_element_type=jnp.float32,
            )
            outgoing[p][k, :, a_index] = rows.astype(jnp.bfloat16).reshape(8, 16, size)
            return carry

        lax.fori_loop(0, RING, one, 0)

    def deliver(p, k, b_step):
        order = ORDERS[p]
        a, b, s = order
        start, size = parts[p]
        b_index = here.along(b, b_step)
        mine = slots_of(slots, order, b_index, here.at[s], here.core, start, size)
        way = 1 if k % 2 == 0 else -1
        wires.send(
            outgoing[p].at[k, pl.ds(here.along(s, 2) * 2, 2)],
            relay[p].at[k],
            here.near(s, way),
            (p, "relay", k),
        )
        for step in (1, -1):
            for other in (0, 1):
                core = 1 - here.core if other else here.core
                wires.send(
                    outgoing[p].at[k, here.along(s, step) * 2 + core],
                    mine,
                    here.near(s, step, other),
                    (p, "near", step, other, k),
                )
        wires.send(
            outgoing[p].at[k, here.at[s] * 2 + (1 - here.core)],
            mine,
            here.partner(),
            (p, "chip", k),
        )
        keep(outgoing[p].at[k, here.at[s] * 2 + here.core], mine)

    def forward(p, k, b_step):
        order = ORDERS[p]
        a, b, s = order
        start, size = parts[p]
        b_index = here.along(b, b_step)
        way = 1 if k % 2 == 0 else -1
        wires.arrived(relay[p].at[k], (p, "relay", k), here.near(s, -way))
        theirs = slots_of(slots, order, b_index, here.along(s, -way), here.core, start, size)
        for other in (0, 1):
            core = 1 - here.core if other else here.core
            wires.send(
                relay[p].at[k, core], theirs, here.near(s, way, other), (p, "far", other, k)
            )

    def received(p, k, b_step):
        order = ORDERS[p]
        a, b, s = order
        start, size = parts[p]
        b_index = here.along(b, b_step)
        way = 1 if k % 2 == 0 else -1
        for other in (0, 1):
            core = 1 - here.core if other else here.core
            for step in (1, -1):
                wires.arrived(
                    slots_of(slots, order, b_index, here.along(s, -step), core, start, size),
                    (p, "near", step, other, k),
                    here.near(s, -step, other),
                )
            wires.arrived(
                slots_of(slots, order, b_index, here.along(s, 2), core, start, size),
                (p, "far", other, k),
                here.near(s, -way, other),
            )
        wires.arrived(
            slots_of(slots, order, b_index, here.at[s], 1 - here.core, start, size),
            (p, "chip", k),
            here.partner(),
        )

    def batch_copy(p, k):
        start, size = parts[p]
        b_index = here.along(ORDERS[p][1], turns[k])
        slot = (k * 3 + p) % 2
        return pltpu.make_async_copy(
            slots.at[(*fixed_b(ORDERS[p], b_index), slice(None), slice(None), pl.ds(start, size))],
            batch.at[slot, :, :, :, :, pl.ds(0, size)],
            bs.at[slot],
        )

    def ready(p, k):
        received(p, k, turns[k])
        local[6 + k * 3 + p].wait()
        batch_copy(p, k).start()

    def project(p, k):
        start, size = parts[p]
        b_index = here.along(ORDERS[p][1], turns[k])
        slot = (k * 3 + p) % 2
        batch_copy(p, k).wait()
        where = fixed_b(ORDERS[p], b_index)

        def tile(n, carry):
            units = pl.ds(pl.multiple_of(n * 256, 256), 256)
            term = lax.dot_general(
                batch[slot, :, :, :, :, pl.ds(0, size)].reshape(512, size),
                weight[units, pl.ds(start, size)],
                (((1,), (1,)), ((), ())),
                preferred_element_type=jnp.float32,
            )
            there = (*where, slice(None), slice(None), units)
            upstream[there] = upstream[there] + term.reshape(RING, RING, 2, 16, 256)
            return carry

        lax.fori_loop(0, 3, tile, 0)

    turns = (0, -1, 1, 2)
    for p in range(3):
        relay_on(p, 0, 0)
    for p in range(3):
        select(p, 0, 0)
        deliver(p, 0, 0)
    for k, step in ((1, -1), (2, 1), (3, 2)):
        for p in range(3):
            relay_on(p, k, step)
    for k in (1, 2):
        for p in range(3):
            select(p, k, turns[k])
            deliver(p, k, turns[k])
    for p in range(3):
        forward(p, 0, 0)
    for p in range(3):
        for k, step in ((0, 0), (1, -1), (2, 1), (3, 2)):
            far_in(p, k, step)
    for p, (a, b, s) in enumerate(ORDERS):
        wires.arrived(seen.at[p, here.along(b, 2)], (p, "t2far"), here.near(b, -1))
    for p in range(3):
        select(p, 3, 2)
        deliver(p, 3, 2)
    maps_out[...] = seen[...]
    upstream[...] = jnp.zeros_like(upstream)
    fetch.wait()
    for p in range(3):
        forward(p, 1, turns[1])
    work = [(k, p) for k in range(4) for p in range(3)]
    ready(work[0][1], work[0][0])
    for turn, (k, p) in enumerate(work):
        if turn + 1 < len(work):
            after_k, after_p = work[turn + 1]
            if after_p == 0 and after_k < 3:
                for q in range(3):
                    forward(q, after_k + 1, turns[after_k + 1])
            ready(after_p, after_k)
        project(p, k)
    wires.drain()


def dispatch(parts, grad, maps, down):
    tokens, width = grad.shape
    rows = [pltpu.VMEM((RING, RING, tokens, size), jnp.bfloat16) for _, size in parts]
    outs = [pltpu.VMEM((RING, 8, RING, 16, size), jnp.bfloat16) for _, size in parts]
    relays = [pltpu.VMEM((RING, 2, RING, 16, size), jnp.bfloat16) for _, size in parts]
    table = (3, RING, RING, 32, LANES)
    units = down.shape[0]
    return pl.pallas_call(
        functools.partial(dispatch_kernel, parts),
        out_shape=(
            jax.ShapeDtypeStruct((RING, RING, RING, 2, 16, width), jnp.bfloat16),
            jax.ShapeDtypeStruct(table, jnp.bfloat16),
            jax.ShapeDtypeStruct((RING, RING, RING, 2, 16, units), jnp.float32),
        ),
        in_specs=[pl.BlockSpec(memory_space=pltpu.HBM)] * 3,
        out_specs=(
            pl.BlockSpec(memory_space=pltpu.HBM),
            pl.BlockSpec(memory_space=pltpu.VMEM),
            pl.BlockSpec(memory_space=pltpu.VMEM),
        ),
        scratch_shapes=rows
        + outs
        + relays
        + [
            pltpu.VMEM(table, jnp.bfloat16),
            pltpu.VMEM((units, width), jnp.bfloat16),
            pltpu.VMEM((2, RING, RING, 2, 16, parts[0][1]), jnp.bfloat16),
            pltpu.SemaphoreType.DMA((192,)),
            pltpu.SemaphoreType.DMA((192,)),
            pltpu.SemaphoreType.DMA((32,)),
            pltpu.SemaphoreType.DMA((3,)),
        ],
        compiler_params=pltpu.CompilerParams(
            collective_id=0, has_side_effects=True, vmem_limit_bytes=60 * 2**20
        ),
    )(grad, maps, down)


def combine_kernel(
    parts, grad_first, grad_second, w_gate, w_up, tables, out, back,
    q0, q1, q2, l0, l1, l2, x0, x1, x2, y0, y1, y2, u0, u1, u2, v0, v1, v2,
    gate, up, stage, ss, rs, ls, bs,
):
    rows, relay = (q0, q1, q2), (l0, l1, l2)
    halves2, whole2 = (x0, x1, x2), (y0, y1, y2)
    halves1, whole1 = (u0, u1, u2), (v0, v1, v2)
    here = Place()
    wires = Wires(ss, rs)
    tokens = out.shape[0]
    local = []
    fetches = []
    for p, (start, size) in enumerate(parts):
        for n, (src, dst) in enumerate(((w_gate, gate), (w_up, up))):
            span = pl.ds(start, size)
            copy = pltpu.make_async_copy(src.at[span], dst.at[span], bs.at[2 + 2 * p + n])
            copy.start()
            fetches.append(copy)
    here.greet()

    def stage_copy(p, k, b_step):
        start, size = parts[p]
        b_index = here.along(ORDERS[p][1], b_step)
        slot = (k * 3 + p) % 2
        return pltpu.make_async_copy(
            stage.at[slot, :, :, :, :, pl.ds(0, size)],
            back.at[(*fixed_b(ORDERS[p], b_index), slice(None), slice(None), pl.ds(start, size))],
            bs.at[slot],
        )

    def produce(p, k, b_step):
        start, size = parts[p]
        b_index = here.along(ORDERS[p][1], b_step)
        slot = (k * 3 + p) % 2
        where = fixed_b(ORDERS[p], b_index)
        units = grad_first.shape[-1]
        if k == 0:
            fetches[2 * p].wait()
            fetches[2 * p + 1].wait()

        def columns(offset, width):
            span = pl.ds(start + offset, width)
            total = 0.0
            for grads, weight in ((grad_first, gate), (grad_second, up)):
                total = total + lax.dot_general(
                    grads[where].reshape(512, units),
                    weight[span],
                    (((1,), (1,)), ((), ())),
                    preferred_element_type=jnp.float32,
                )
            stage[slot, :, :, :, :, pl.ds(offset, width)] = total.astype(jnp.bfloat16).reshape(
                RING, RING, 2, 16, width
            )

        def tile(n, carry):
            columns(pl.multiple_of(n * 256, 256), 256)
            return carry

        lax.fori_loop(0, size // 256, tile, 0)
        if size % 256:
            columns(size // 256 * 256, size % 256)
        stage_copy(p, k, b_step).start()

    def pieces(p, b_index, s_index, c_index):
        start, size = parts[p]
        return slots_of(back, ORDERS[p], b_index, s_index, c_index, start, size)

    def give(p, k, b_step):
        a, b, s = ORDERS[p]
        b_index = here.along(b, b_step)
        mine = rows[p].at[b_index, :, here.at[s] * 2 + here.core]
        way = 1 if k % 2 == 0 else -1
        wires.send(
            pieces(p, b_index, here.along(s, 2), slice(None)),
            relay[p].at[k],
            here.near(s, way),
            (p, "relay", k),
        )
        for step in (1, -1):
            for other in (0, 1):
                core = 1 - here.core if other else here.core
                wires.send(
                    pieces(p, b_index, here.along(s, step), core),
                    mine,
                    here.near(s, step, other),
                    (p, "near", step, other, k),
                )
        wires.send(
            pieces(p, b_index, here.at[s], 1 - here.core), mine, here.partner(), (p, "chip", k)
        )
        copy = pltpu.make_async_copy(
            pieces(p, b_index, here.at[s], here.core), mine, ls.at[len(local)]
        )
        copy.start()
        local.append(copy)

    def forward(p, k, b_step):
        a, b, s = ORDERS[p]
        b_index = here.along(b, b_step)
        way = 1 if k % 2 == 0 else -1
        wires.arrived(relay[p].at[k], (p, "relay", k), here.near(s, -way))
        theirs = rows[p].at[b_index, :, here.along(s, -way) * 2 + here.core]
        for other in (0, 1):
            core = 1 - here.core if other else here.core
            wires.send(
                relay[p].at[k, :, core], theirs, here.near(s, way, other), (p, "far", other, k)
            )

    def gathered(p, k, b_step):
        a, b, s = ORDERS[p]
        b_index = here.along(b, b_step)
        way = 1 if k % 2 == 0 else -1
        for other in (0, 1):
            core = 1 - here.core if other else here.core
            for step in (1, -1):
                wires.arrived(
                    rows[p].at[b_index, :, here.along(s, -step) * 2 + core],
                    (p, "near", step, other, k),
                    here.near(s, -step, other),
                )
            wires.arrived(
                rows[p].at[b_index, :, here.along(s, 2) * 2 + core],
                (p, "far", other, k),
                here.near(s, -way, other),
            )
        wires.arrived(
            rows[p].at[b_index, :, here.at[s] * 2 + (1 - here.core)],
            (p, "chip", k),
            here.partner(),
        )
        local[k * 3 + p].wait()

    def add_up(p, b_step):
        a, b, s = ORDERS[p]
        b_index = here.along(b, b_step)
        line = here.at[b] * RING + here.at[a]
        size = parts[p][1]

        def one(a_index, carry):
            token_of = line_row(tables[p, b_index, a_index, pl.ds(0, 16), :], line)
            gate_of = line_row(tables[p, b_index, a_index, pl.ds(16, 16), :], line)
            token = lax.broadcasted_iota(jnp.int32, (tokens, LANES), 0).astype(jnp.float32)
            weigh = jnp.where(token == token_of, gate_of, 0.0).astype(jnp.bfloat16)
            total = jnp.dot(
                weigh,
                rows[p][b_index, a_index].reshape(LANES, size),
                preferred_element_type=jnp.float32,
            )
            rows[p][b_index, a_index] = total.astype(jnp.bfloat16).reshape(8, 16, size)
            return carry

        lax.fori_loop(0, RING, one, 0)

    def plus(*terms):
        total = terms[0].astype(jnp.float32)
        for term in terms[1:]:
            total = total + term.astype(jnp.float32)
        return total

    def fold2(p, way):
        a, b, s = ORDERS[p]
        b_index = here.along(b, way)
        slot = 0 if way == 1 else 1
        groups = pl.ds(0, 4) if way == 1 else pl.ds(4, 4)
        wires.arrived(halves2[p].at[slot], (p, "half2", way), here.near(b, -way))

        def one(a_index, carry):
            rows[p][b_index, a_index, groups] = plus(
                rows[p][b_index, a_index, groups], halves2[p][slot, a_index]
            ).astype(jnp.bfloat16)
            return carry

        lax.fori_loop(0, RING, one, 0)
        for k, step in enumerate((2, 1, -1, 0)):
            wires.send(
                rows[p].at[b_index, here.along(a, step)],
                whole2[p].at[slot, k],
                here.near(b, way),
                (p, "whole2", way, k),
            )

    def settle2(p, k, step):
        a, b, s = ORDERS[p]
        for way in (1, -1):
            slot = 0 if way == 1 else 1
            wires.arrived(whole2[p].at[slot, k], (p, "whole2", way, k), here.near(b, -way))
        own = rows[p].at[here.at[b], here.along(a, step)]
        return plus(own[...], whole2[p][0, k], whole2[p][1, k])

    order = (2, 1, -1, 0)
    work = [(k, p) for k in range(4) for p in range(3)]
    for turn in range(len(work) + 1):
        if turn < len(work):
            k, p = work[turn]
            produce(p, k, order[k])
        if turn > 0:
            k, p = work[turn - 1]
            stage_copy(p, k, order[k]).wait()
            give(p, k, order[k])
            if p == 2 and k > 0:
                for q in range(3):
                    forward(q, k - 1, order[k - 1])
    for p, (a, b, s) in enumerate(ORDERS):
        gathered(p, 0, 2)
        add_up(p, 2)
        far = here.along(b, 2)
        for way, groups in ((1, pl.ds(0, 4)), (-1, pl.ds(4, 4))):
            wires.send(
                rows[p].at[far, :, groups],
                halves2[p].at[0 if way == 1 else 1],
                here.near(b, way),
                (p, "half2", way),
            )
    for q in range(3):
        forward(q, 3, order[3])
    for k, way in ((1, 1), (2, -1)):
        for p in range(3):
            gathered(p, k, way)
            add_up(p, way)
            fold2(p, way)
    for p in range(3):
        gathered(p, 3, 0)
        add_up(p, 0)
    for p, (a, b, s) in enumerate(ORDERS):
        block = rows[p].at[here.at[b], here.along(a, 2)]
        block[...] = settle2(p, 0, 2).astype(jnp.bfloat16)
        for way, groups in ((1, pl.ds(0, 4)), (-1, pl.ds(4, 4))):
            wires.send(
                rows[p].at[here.at[b], here.along(a, 2), groups],
                halves1[p].at[0 if way == 1 else 1],
                here.near(a, way),
                (p, "half1", way),
            )
    for k, way in ((1, 1), (2, -1)):
        for p, (a, b, s) in enumerate(ORDERS):
            slot = 0 if way == 1 else 1
            groups = pl.ds(0, 4) if way == 1 else pl.ds(4, 4)
            block = rows[p].at[here.at[b], here.along(a, way)]
            block[...] = settle2(p, k, way).astype(jnp.bfloat16)
            wires.arrived(halves1[p].at[slot], (p, "half1", way), here.near(a, -way))
            part = rows[p].at[here.at[b], here.along(a, way), groups]
            part[...] = plus(part[...], halves1[p][slot]).astype(jnp.bfloat16)
            wires.send(block, whole1[p].at[slot], here.near(a, way), (p, "whole1", way))
    for p, (a, b, s) in enumerate(ORDERS):
        start, size = parts[p]
        total = settle2(p, 3, 0)
        for way in (1, -1):
            slot = 0 if way == 1 else 1
            wires.arrived(whole1[p].at[slot], (p, "whole1", way), here.near(a, -way))
        total = plus(total, whole1[p][0], whole1[p][1])
        out[:, pl.ds(start, size)] = total.reshape(tokens, size)
    wires.drain()


def combine(parts, grad_first, grad_second, w_gate, w_up, tables, tokens):
    width, units = w_gate.shape

    def buffers(*lead):
        return [pltpu.VMEM((*lead, size), jnp.bfloat16) for _, size in parts]

    return pl.pallas_call(
        functools.partial(combine_kernel, parts),
        out_shape=(
            jax.ShapeDtypeStruct((tokens, width), jnp.float32),
            jax.ShapeDtypeStruct((RING, RING, RING, 2, 16, width), jnp.bfloat16),
        ),
        in_specs=[
            pl.BlockSpec(memory_space=pltpu.VMEM),
            pl.BlockSpec(memory_space=pltpu.VMEM),
            pl.BlockSpec(memory_space=pltpu.HBM),
            pl.BlockSpec(memory_space=pltpu.HBM),
            pl.BlockSpec(memory_space=pltpu.VMEM),
        ],
        out_specs=(
            pl.BlockSpec(memory_space=pltpu.VMEM),
            pl.BlockSpec(memory_space=pltpu.HBM),
        ),
        scratch_shapes=buffers(RING, RING, 8, 16)
        + buffers(RING, RING, 2, 16)
        + buffers(2, RING, 4, 16)
        + buffers(2, RING, 8, 16)
        + buffers(2, 4, 16)
        + buffers(2, 8, 16)
        + [
            pltpu.VMEM((width, units), jnp.bfloat16),
            pltpu.VMEM((width, units), jnp.bfloat16),
            pltpu.VMEM((2, RING, RING, 2, 16, parts[0][1]), jnp.bfloat16),
            pltpu.SemaphoreType.DMA((192,)),
            pltpu.SemaphoreType.DMA((192,)),
            pltpu.SemaphoreType.DMA((16,)),
            pltpu.SemaphoreType.DMA((8,)),
        ],
        compiler_params=pltpu.CompilerParams(
            collective_id=1, has_side_effects=True, vmem_limit_bytes=63 * 2**20
        ),
    )(grad_first, grad_second, w_gate, w_up, tables)[0]


def in_blocks(shard, dim, size):
    shape = shard.shape
    parts = shard.reshape(*shape[:dim], size, shape[dim] // size, *shape[dim + 1 :])
    return jnp.moveaxis(parts, dim, 0)


def summed_on_arrival(shard, axis, dim):
    size = lax.axis_size(axis)
    parts = lax.all_to_all(in_blocks(shard, dim, size), axis, 0, 0, tiled=True)
    return jnp.sum(parts, axis=0)


def hidden_backward(upstream, pre_gate, pre_up):
    first = pre_gate.astype(jnp.float32)
    second = pre_up.astype(jnp.float32)
    gate_sig = jax.nn.sigmoid(first)
    gate_act = first * gate_sig
    hidden = gate_act * second
    slot_combine = jnp.sum(upstream * hidden, axis=-1).astype(jnp.bfloat16)
    grad_first = (upstream * second * gate_sig * (1.0 + first * (1.0 - gate_sig))).astype(
        jnp.bfloat16
    )
    grad_second = (upstream * gate_act).astype(jnp.bfloat16)
    return grad_first, grad_second, slot_combine


def shards(
    tokens,
    out_grad,
    router_weight,
    gate_weight,
    up_weight,
    down_weight,
    saved_gate,
    saved_up,
    expert_ids,
    aux_weight,
):
    devices = lax.axis_size(AXES)
    seq_size = lax.axis_size(SEQ)
    inputs, upstream_grad, chosen_ids = tokens[0], out_grad[0], expert_ids[0]
    tok_rows, top_count = chosen_ids.shape
    model_width = inputs.shape[1]
    experts = router_weight.shape[1]
    capacity = saved_gate.shape[1] // devices
    parts = column_parts(model_width)

    logits = jnp.dot(inputs, router_weight, preferred_element_type=jnp.float32)
    probs = jax.nn.softmax(logits, axis=-1)
    expert = jnp.arange(experts, dtype=jnp.int32)
    mask = jnp.sum((chosen_ids[:, :, None] == expert).astype(jnp.float32), axis=1)
    chosen_sum = jnp.sum(probs * mask, axis=1, keepdims=True)
    gates = probs * mask / chosen_sum
    position = jnp.arange(tok_rows)
    before = (position[:, None] > position[None, :]).astype(jnp.bfloat16)
    slot_pos = jnp.dot(before, mask.astype(jnp.bfloat16), preferred_element_type=jnp.float32)
    slot = jnp.arange(capacity, dtype=jnp.float32)
    filled = jnp.where(
        (slot_pos[:, None, :] == slot[None, :, None]) & (mask[:, None, :] > 0), 1.0, 0.0
    )
    offset = (position - tok_rows).astype(jnp.float32)
    slot_token = jnp.sum(filled * offset[:, None, None], axis=0) + tok_rows
    slot_gate = jnp.sum(filled * gates[:, None, :], axis=0)
    tables = []
    for a, b, s in ORDERS:
        both = jnp.stack([slot_token, slot_gate]).reshape(2, capacity, RING, RING, RING, 2)
        both = both.transpose(0, 2 + b, 2 + a, 2 + s, 5, 1)
        tables.append(both.reshape(2 * RING * RING, LANES))
    tables = jnp.stack(tables).astype(jnp.bfloat16)

    _, seen, upstream = dispatch(parts, upstream_grad, tables, down_weight[0])
    grad_first, grad_second, slot_combine = hidden_backward(
        upstream,
        saved_gate[0].reshape(upstream.shape),
        saved_up[0].reshape(upstream.shape),
    )
    combine_back = lax.all_to_all(
        slot_combine.reshape(1, devices, capacity), AXES, split_axis=1, concat_axis=0, tiled=True
    ).reshape(experts, capacity)
    expert_sum = combine(
        parts, grad_first, grad_second, gate_weight[0], up_weight[0], seen, tok_rows
    )

    in_seq = seen[0, :, :, : RING * RING].astype(jnp.float32)
    used = jnp.sum((in_seq < tok_rows).astype(jnp.float32), axis=(0, 1))
    used = jnp.sum(used.reshape(RING, RING, RING, 2, capacity), axis=-1)
    seq_counts = used.transpose(1, 0, 2, 3).reshape(experts)

    combine_dense = jnp.sum(filled * combine_back.T.astype(jnp.float32)[None], axis=1)
    combine_grad = jnp.sum(
        jnp.where(chosen_ids[:, :, None] == expert, combine_dense[:, None, :], 0.0), axis=-1
    )
    prob_sel = (
        combine_dense - jnp.sum(gates * combine_dense, axis=1, keepdims=True)
    ) / chosen_sum
    fraction = experts * seq_counts / (top_count * tok_rows * seq_size)
    prob_grad = prob_sel * mask + aux_weight[0] * fraction[None, :]
    dlogits = probs * (prob_grad - jnp.sum(probs * prob_grad, axis=1, keepdims=True))
    logit_grad = dlogits.astype(jnp.bfloat16)
    token_grad = expert_sum + jnp.einsum(
        "te,de->td", logit_grad, router_weight, preferred_element_type=jnp.float32
    )
    router = jnp.einsum("td,te->de", inputs, logit_grad, preferred_element_type=jnp.float32)
    for axis in AXES:
        router = summed_on_arrival(router, axis, 0)
    return (token_grad.astype(jnp.bfloat16)[None], combine_grad[None], router)


def solution(mesh):
    torus = Mesh(mesh.devices.reshape(RING, RING, RING, 2), AXES)
    return jax.shard_map(
        shards,
        mesh=torus,
        in_specs=(
            P(EXP, SEQ, None),
            P(EXP, SEQ, None),
            P(),
            P(AXES, None, None),
            P(AXES, None, None),
            P(AXES, None, None),
            P(AXES, None, None),
            P(AXES, None, None),
            P(EXP, SEQ, None),
            P(),
        ),
        out_specs=(P(EXP, SEQ, None), P(EXP, SEQ, None), P(AXES, None)),
        check_vma=False,
    )
```

profile of v0, /device:TPU:82, one launch (start us, length us, event | category | flops | bytes accessed | tf_op | source)
XLA Modules:
  0.0 378.9 jit_solution(17546550210744860265)
XLA Ops:
  0.6 0.8 copy.85
  1.4 0.2 convert_reduce_fusion
  1.8 0.1 fusion.19
  1.9 2.1 fusion.25
  4.2 0.3 fusion.11
  5.7 0.6 pad_maximum_fusion.maps
  6.3 145.0 %shard_map.121 = (bf16[4,4,4,2,16,4096]{5,4,3,2,1,0:T(8,128)(2,1)}, bf16[3,4,4,32,128]{4,3,2,1,0:T(8,128)(2,1)}, f32[4,4,4,2,16,768]{5,4,3,2,1,0:T(8,128)}) custom-call(bf16[128,4096]{1,0:T(8,128)(2,1)} %bitcast.58, bf16[3,32,128]{2,1,0:T(8,128)(2,1)} %pad_maximum_fusion.maps, bf16[768,4096]{1,0:T(8,128)(2,1)} %bitcast.52), custom_call_target="tpu_custom_call" | custom-call | tf_op jit(solution)/shard_map/pallas_call | solution.py:364
  151.3 9.9 %fusion.4 = (bf16[4,4,4,2,16]{4,3,2,1,0:T(2,128)(2,1)S(1)}, bf16[4,4,4,2,16,768]{5,4,3,2,1,0:T(8,128)(2,1)}, bf16[4,4,4,2,16,768]{5,4,3,2,1,0:T(8,128)(2,1)}) fusion(f32[4,4,4,2,16,768]{5,4,3,2,1,0:T(8,128)} %get-tuple-element.6, bf16[4,4,4,2,16,768]{5,4,3,2,1,0:T(8,128)(2,1)} %bitcast.55, bf16[4,4,4,2,16,768]{5,4,3,2,1,0:T(8,128)(2,1)} %bitcast.56), kind=kLoop, calls=%fused_computation.9 | loop fusion | flops 28309504 | bytes 18878464 | tf_op jit(solution)/shard_map/reduce_sum | solution.py:712
  161.2 0.7 copy.93
  161.9 9.9 %all-to-all-start = ((bf16[1,128,16]{2,0,1:T(2,128)(2,1)}), bf16[1,128,16]{2,0,1:T(2,128)(2,1)S(1)}, u32[]{:S(2)}, u32[]{:S(2)}) async-start(bf16[1,128,16]{2,0,1:T(2,128)(2,1)} %copy.93), calls=%async_computation | async-start | bytes 131072 | tf_op jit(solution)/shard_map/all_to_all | solution.py:770
  172.4 0.9 convert_reduce_fusion.1
  173.4 0.2 reduce_sum.153
  173.6 0.2 copy.111
  173.8 0.2 copy.99
  174.0 0.1 mul.110
  174.2 2.7 all-to-all-done
  177.1 0.5 fusion.13
  177.9 0.4 fusion.14
  178.3 0.2 copy.114
  178.5 28.5 %all_to_all.29 = f32[4,1024,128]{1,2,0:T(8,128)S(1)} all-to-all(f32[4,1024,128]{1,2,0:T(8,128)S(1)} %bitcast.50), channel_id=1, replica_groups=mesh['seq_0'=4,'seq_1'=4,'exp_0'=4,'exp_1'=2] {'seq_0'}, dimensions={0} | all-to-all | bytes 4194304 | tf_op jit(solution)/shard_map/all_to_all | solution.py:702
  207.0 0.2 reduce_sum.156
  207.2 0.8 copy.115
  208.0 4.9 %all-to-all-start.2 = ((f32[4,256,128]{1,2,0:T(8,128)}), f32[4,256,128]{1,2,0:T(8,128)S(1)}, u32[]{:S(2)}, u32[]{:S(2)}) async-start(f32[4,256,128]{1,2,0:T(8,128)} %bitcast.47), calls=%async_computation.2 | async-start | bytes 1048576 | tf_op jit(solution)/shard_map/all_to_all | solution.py:702
  212.9 148.7 %shard_map.122 = (f32[128,4096]{1,0:T(8,128)}, bf16[4,4,4,2,16,4096]{5,4,3,2,1,0:T(8,128)(2,1)}) custom-call(bf16[4,4,4,2,16,768]{5,4,3,2,1,0:T(8,128)(2,1)} %get-tuple-element.18.grad_first, bf16[4,4,4,2,16,768]{5,4,3,2,1,0:T(8,128)(2,1)} %get-tuple-element.19.grad_second, bf16[4096,768]{1,0:T(8,128)(2,1)} %bitcast.53, bf16[4096,768]{1,0:T(8,128)(2,1)} %bitcast.54, ...), custom_call_target="tpu_custom_call" | custom-call | tf_op jit(solution)/shard_map/pallas_call | solution.py:656
  361.7 3.4 fusion.10
  365.1 0.7 copy.104
  365.8 5.4 %all-to-all-start.3 = ((f32[4,64,128]{2,1,0:T(8,128)}), f32[4,64,128]{2,1,0:T(8,128)S(1)}, u32[]{:S(2)}, u32[]{:S(2)}) async-start(f32[4,64,128]{2,1,0:T(8,128)} %bitcast.23), calls=%async_computation.3 | async-start | bytes 262144 | tf_op jit(solution)/shard_map/all_to_all | solution.py:702
  371.2 0.4 select_reduce_fusion
  371.6 0.7 copy.105
  372.3 2.2 all-to-all-done.3
  374.5 3.7 all_to_all.30
  378.3 0.6 reduce_sum.159
  (32 shorter events, 2.0 us)
Async XLA Ops:
  151.2 26.6 %copy-start = (bf16[1,128,4096]{2,1,0:T(8,128)(2,1)S(1)}, bf16[1,128,4096]{2,1,0:T(8,128)(2,1)}, u32[]{:S(2)}) copy-start(bf16[1,128,4096]{2,1,0:T(8,128)(2,1)} %param.10) | copy-start | bytes 3145732
  161.9 15.1 %all-to-all-start = ((bf16[1,128,16]{2,0,1:T(2,128)(2,1)}), bf16[1,128,16]{2,0,1:T(2,128)(2,1)S(1)}, u32[]{:S(2)}, u32[]{:S(2)}) async-start(bf16[1,128,16]{2,0,1:T(2,128)(2,1)} %copy.93), calls=%async_computation | async-start | bytes 131072 | tf_op jit(solution)/shard_map/all_to_all | solution.py:770
  208.0 157.0 %all-to-all-start.2 = ((f32[4,256,128]{1,2,0:T(8,128)}), f32[4,256,128]{1,2,0:T(8,128)S(1)}, u32[]{:S(2)}, u32[]{:S(2)}) async-start(f32[4,256,128]{1,2,0:T(8,128)} %bitcast.47), calls=%async_computation.2 | async-start | bytes 1048576 | tf_op jit(solution)/shard_map/all_to_all | solution.py:702
  365.8 8.7 %all-to-all-start.3 = ((f32[4,64,128]{2,1,0:T(8,128)}), f32[4,64,128]{2,1,0:T(8,128)S(1)}, u32[]{:S(2)}, u32[]{:S(2)}) async-start(f32[4,64,128]{2,1,0:T(8,128)} %bitcast.23), calls=%async_computation.3 | async-start | bytes 262144 | tf_op jit(solution)/shard_map/all_to_all | solution.py:702
where the time goes:
time: 384 us; the launch traced here: 379 us
  Pallas kernels  294 us (77%)
  blocking collectives  32.2 us (8%)
  starting transfers between devices  20.2 us (5%)
  other arithmetic  14.6 us (4%)
  matrix products  5.99 us (2%)
  local copies, waits for them, and re-layouts  5.66 us (1%)
  waiting for transfers between devices  4.98 us (1%)
    pallas_call x1, Pallas kernels, combine(): pl.pallas_call(functools.partial(combine_kernel, parts), out_shape=(jax.S...  149 us
    pallas_call x1, Pallas kernels, dispatch(): pl.pallas_call(functools.partial(dispatch_kernel, parts), out_shape=(jax....  145 us
    all_to_all x2, blocking collectives, summed_on_arrival(): parts = lax.all_to_all(in_blocks(shard, dim, size), axis, 0, 0, tiled=True)  32.2 us
    all_to_all x2, starting transfers between devices, summed_on_arrival(): parts = lax.all_to_all(in_blocks(shard, dim, size), axis, 0, 0, tiled=True)  10.3 us
    all_to_all x1, starting transfers between devices, shards(): lax.all_to_all(slot_combine.reshape(1, devices, capacity), AXES, split_ax...  9.93 us
    reduce_sum x1, other arithmetic, hidden_backward(): slot_combine = jnp.sum(upstream * hidden, axis=-1).astype(jnp.bfloat16)  9.91 us
  transfers between devices with their start and end apart: 3, of which 2 were waited for; matrix products, arithmetic and copies ran while one was open for 2% of the time, Pallas kernels for 39%

commit v1 on v0

--- a/solution.py
+++ b/solution.py
@@ -67,11 +67,11 @@
     def partner(self):
         return (self.at[0], self.at[1], self.at[2], 1 - self.core)
 
-    def greet(self):
+    def greet(self, steps=(1, -1)):
         barrier = pltpu.get_barrier_semaphore()
         peers = [self.partner()]
         for axis in range(3):
-            for step in (1, -1):
+            for step in steps:
                 for other in (0, 1):
                     peers.append(self.near(axis, step, other))
         for peer in peers:
@@ -359,7 +359,7 @@
     rows = [pltpu.VMEM((RING, RING, tokens, size), jnp.bfloat16) for _, size in parts]
     outs = [pltpu.VMEM((RING, 8, RING, 16, size), jnp.bfloat16) for _, size in parts]
     relays = [pltpu.VMEM((RING, 2, RING, 16, size), jnp.bfloat16) for _, size in parts]
-    table = (3, RING, RING, 32, LANES)
+    table = (3, RING, RING, maps.shape[1], LANES)
     units = down.shape[0]
     return pl.pallas_call(
         functools.partial(dispatch_kernel, parts),
@@ -393,13 +393,19 @@
 
 
 def combine_kernel(
-    parts, grad_first, grad_second, w_gate, w_up, tables, out, back,
+    parts, values, grad_first, grad_second, w_gate, w_up, tables, inputs, router,
+    probs, gates, place, scale, ids, aux,
+    out, combine_grad, router_grad, back,
     q0, q1, q2, l0, l1, l2, x0, x1, x2, y0, y1, y2, u0, u1, u2, v0, v1, v2,
-    gate, up, stage, ss, rs, ls, bs,
+    gate, up, stage, given, h1, h2, h3, flat, logit_grad, terms, other_terms,
+    e10, e11, e12, e20, e21, e22, e30, e31, e32, ss, rs, ls, bs,
 ):
     rows, relay = (q0, q1, q2), (l0, l1, l2)
     halves2, whole2 = (x0, x1, x2), (y0, y1, y2)
     halves1, whole1 = (u0, u1, u2), (v0, v1, v2)
+    sums = ((e10, e11, e12), (e20, e21, e22), (e30, e31, e32))
+    bands = ((0, 16), (16, 8), (24, 8))
+    steps = (1, -1, 2)
     here = Place()
     wires = Wires(ss, rs)
     tokens = out.shape[0]
@@ -408,10 +414,160 @@
     for p, (start, size) in enumerate(parts):
         for n, (src, dst) in enumerate(((w_gate, gate), (w_up, up))):
             span = pl.ds(start, size)
-            copy = pltpu.make_async_copy(src.at[span], dst.at[span], bs.at[2 + 2 * p + n])
+            copy = pltpu.make_async_copy(src.at[span], dst.at[span], bs.at[6 + 2 * p + n])
             copy.start()
             fetches.append(copy)
-    here.greet()
+
+    def given_copies(p, k, b_step):
+        slot = (k * 3 + p) % 2
+        where = fixed_b(ORDERS[p], here.along(ORDERS[p][1], b_step))
+        return [
+            pltpu.make_async_copy(src.at[where], given.at[slot, n], bs.at[2 + 2 * slot + n])
+            for n, src in enumerate((grad_first, grad_second))
+        ]
+
+    for copy in given_copies(0, 0, 2):
+        copy.start()
+    here.greet(steps)
+
+    def values_line():
+        mine = here.at[2] * 2 + here.core
+        h1[mine] = values[:, :, here.at[2], here.core]
+        for step in (0, *steps):
+            for other in (0, 1):
+                if step or other:
+                    core = 1 - here.core if other else here.core
+                    wires.send(
+                        values.at[:, :, here.along(2, step), core],
+                        h1.at[mine],
+                        here.near(2, step, other),
+                        ("v1", step, other),
+                    )
+
+    def values_x():
+        for step in (0, *steps):
+            for other in (0, 1):
+                if step or other:
+                    core = 1 - here.core if other else here.core
+                    wires.arrived(
+                        h1.at[here.along(2, -step) * 2 + core],
+                        ("v1", step, other),
+                        here.near(2, -step, other),
+                    )
+        h2[here.at[1]] = h1[:, :, here.at[1]]
+        for step in steps:
+            wires.send(
+                h1.at[:, :, here.along(1, step)],
+                h2.at[here.at[1]],
+                here.near(1, step),
+                ("v2", step),
+            )
+
+    def values_z():
+        for step in steps:
+            wires.arrived(h2.at[here.along(1, -step)], ("v2", step), here.near(1, -step))
+        h3[here.at[0]] = h2[:, :, here.at[0]]
+        for step in steps:
+            wires.send(
+                h2.at[:, :, here.along(0, step)],
+                h3.at[here.at[0]],
+                here.near(0, step),
+                ("v3", step),
+            )
+
+    def router_back():
+        for step in steps:
+            wires.arrived(h3.at[here.along(0, -step)], ("v3", step), here.near(0, -step))
+
+        def one_expert(e, carry):
+            flat[pl.ds(e, 1), :] = h3[e // 32, (e // 8) % 4, e % 8]
+            return carry
+
+        lax.fori_loop(0, flat.shape[0], one_expert, 0)
+        by_slot = flat[...].T
+        dense = jnp.zeros_like(by_slot)
+        for j in range(16):
+            dense = dense + jnp.where(place[...] == j, by_slot[j : j + 1], 0.0)
+        lane = lax.broadcasted_iota(jnp.int32, dense.shape, 1)
+        column = lax.broadcasted_iota(jnp.int32, combine_grad.shape, 1)
+        picked = jnp.zeros(combine_grad.shape, jnp.float32)
+        for k in range(combine_grad.shape[1]):
+            value = jnp.sum(
+                jnp.where(lane == ids[:, k : k + 1], dense, 0.0), axis=1, keepdims=True
+            )
+            picked = picked + jnp.where(column == k, value, 0.0)
+        combine_grad[...] = picked
+        inner = jnp.sum(gates[...] * dense, axis=1, keepdims=True)
+        prob_grad = jnp.where(place[...] >= 0, (dense - inner) / scale[...], 0.0)
+        counts = jnp.sum(tables[0, :, :, pl.ds(32, 16), :].astype(jnp.float32), axis=(0, 1))
+        counts = jnp.sum(counts, axis=0, keepdims=True)
+        top = combine_grad.shape[1]
+        fraction = dense.shape[1] * counts / (top * tokens * RING * RING)
+        prob_grad = prob_grad + aux[0] * fraction
+        mean = jnp.sum(probs[...] * prob_grad, axis=1, keepdims=True)
+        logit_grad[...] = (probs[...] * (prob_grad - mean)).astype(jnp.bfloat16)
+
+        def one_tile(n, carry):
+            columns = pl.ds(pl.multiple_of(n * LANES, LANES), LANES)
+            term = lax.dot_general(
+                inputs[:, columns],
+                logit_grad[...],
+                (((0,), (0,)), ((), ())),
+                preferred_element_type=jnp.float32,
+            )
+            for m in range(2):
+                for core in range(2):
+                    terms[core, n // 8, (n // 2) % 4, 2 * (n % 2) + m] = term[
+                        64 * m + 32 * core : 64 * m + 32 * core + 32
+                    ]
+            return carry
+
+        lax.fori_loop(0, inputs.shape[1] // LANES, one_tile, 0)
+        wires.send(terms.at[1 - here.core], other_terms, here.partner(), ("r0",))
+
+    def chip_sum():
+        wires.arrived(other_terms, ("r0",), here.partner())
+
+        def one(n, carry):
+            z, x = n // RING, n % RING
+            terms[here.core, z, x] = terms[here.core, z, x] + other_terms[z, x]
+            return carry
+
+        lax.fori_loop(0, RING * RING, one, 0)
+
+    def band_of(q, level, coordinate):
+        where = [slice(None)] * 3
+        for axis in ORDERS[q][:level]:
+            where[axis] = here.at[axis]
+        where[ORDERS[q][level]] = coordinate
+        return (here.core, *where, pl.ds(*bands[q]), slice(None))
+
+    def sum_send(level):
+        for q in range(3):
+            axis = ORDERS[q][level]
+            for n, step in enumerate(steps):
+                wires.send(
+                    terms.at[band_of(q, level, here.along(axis, step))],
+                    sums[level][q].at[n],
+                    here.near(axis, step),
+                    ("r", level, q, step),
+                )
+
+    def sum_in(level):
+        for q in range(3):
+            axis = ORDERS[q][level]
+            for n, step in enumerate(steps):
+                wires.arrived(
+                    sums[level][q].at[n], ("r", level, q, step), here.near(axis, -step)
+                )
+            own = band_of(q, level, here.at[axis])
+            landed = sums[level][q]
+            terms[own] = terms[own] + landed[0] + landed[1] + landed[2]
+
+    def sum_out():
+        for q in range(3):
+            span = pl.ds(*bands[q])
+            router_grad[span] = terms[here.core, here.at[0], here.at[1], here.at[2], span]
 
     def stage_copy(p, k, b_step):
         start, size = parts[p]
@@ -427,18 +583,19 @@
         start, size = parts[p]
         b_index = here.along(ORDERS[p][1], b_step)
         slot = (k * 3 + p) % 2
-        where = fixed_b(ORDERS[p], b_index)
         units = grad_first.shape[-1]
         if k == 0:
             fetches[2 * p].wait()
             fetches[2 * p + 1].wait()
+        for copy in given_copies(p, k, b_step):
+            copy.wait()
 
         def columns(offset, width):
             span = pl.ds(start + offset, width)
             total = 0.0
-            for grads, weight in ((grad_first, gate), (grad_second, up)):
+            for n, weight in enumerate((gate, up)):
                 total = total + lax.dot_general(
-                    grads[where].reshape(512, units),
+                    given[slot, n].reshape(512, units),
                     weight[span],
                     (((1,), (1,)), ((), ())),
                     preferred_element_type=jnp.float32,
@@ -584,9 +741,15 @@
 
     order = (2, 1, -1, 0)
     work = [(k, p) for k in range(4) for p in range(3)]
+    values_line()
+    between = {2: values_x, 4: values_z, 6: router_back, 8: chip_sum}
     for turn in range(len(work) + 1):
         if turn < len(work):
             k, p = work[turn]
+            if turn + 1 < len(work):
+                after_k, after_p = work[turn + 1]
+                for copy in given_copies(after_p, after_k, order[after_k]):
+                    copy.start()
             produce(p, k, order[k])
         if turn > 0:
             k, p = work[turn - 1]
@@ -595,6 +758,10 @@
             if p == 2 and k > 0:
                 for q in range(3):
                     forward(q, k - 1, order[k - 1])
+        if turn in between:
+            between[turn]()
+        if turn == 8:
+            sum_send(0)
     for p, (a, b, s) in enumerate(ORDERS):
         gathered(p, 0, 2)
         add_up(p, 2)
@@ -613,6 +780,8 @@
             gathered(p, k, way)
             add_up(p, way)
             fold2(p, way)
+        sum_in(k - 1)
+        sum_send(k)
     for p in range(3):
         gathered(p, 3, 0)
         add_up(p, 0)
@@ -642,34 +811,44 @@
         for way in (1, -1):
             slot = 0 if way == 1 else 1
             wires.arrived(whole1[p].at[slot], (p, "whole1", way), here.near(a, -way))
-        total = plus(total, whole1[p][0], whole1[p][1])
-        out[:, pl.ds(start, size)] = total.reshape(tokens, size)
+        total = plus(total, whole1[p][0], whole1[p][1]).reshape(tokens, size)
+        total = total + lax.dot_general(
+            logit_grad[...],
+            router[pl.ds(start, size)],
+            (((1,), (1,)), ((), ())),
+            preferred_element_type=jnp.float32,
+        )
+        out[:, pl.ds(start, size)] = total.astype(out.dtype)
+    sum_in(2)
+    sum_out()
     wires.drain()
 
 
-def combine(parts, grad_first, grad_second, w_gate, w_up, tables, tokens):
-    width, units = w_gate.shape
+def combine(parts, values, grads, weights, tables, inputs, router, probs, gates, place, scale, ids, aux):
+    width, units = weights[0].shape
+    tokens, top = ids.shape
+    experts = probs.shape[1]
 
     def buffers(*lead):
         return [pltpu.VMEM((*lead, size), jnp.bfloat16) for _, size in parts]
 
+    def floats(*shape):
+        return pltpu.VMEM(shape, jnp.float32)
+
+    hbm, vmem = pl.BlockSpec(memory_space=pltpu.HBM), pl.BlockSpec(memory_space=pltpu.VMEM)
+    bands = (16, 8, 8)
     return pl.pallas_call(
         functools.partial(combine_kernel, parts),
         out_shape=(
-            jax.ShapeDtypeStruct((tokens, width), jnp.float32),
+            jax.ShapeDtypeStruct((tokens, width), jnp.bfloat16),
+            jax.ShapeDtypeStruct((tokens, top), jnp.float32),
+            jax.ShapeDtypeStruct((width // (2 * RING**3), experts), jnp.float32),
             jax.ShapeDtypeStruct((RING, RING, RING, 2, 16, width), jnp.bfloat16),
         ),
-        in_specs=[
-            pl.BlockSpec(memory_space=pltpu.VMEM),
-            pl.BlockSpec(memory_space=pltpu.VMEM),
-            pl.BlockSpec(memory_space=pltpu.HBM),
-            pl.BlockSpec(memory_space=pltpu.HBM),
-            pl.BlockSpec(memory_space=pltpu.VMEM),
-        ],
-        out_specs=(
-            pl.BlockSpec(memory_space=pltpu.VMEM),
-            pl.BlockSpec(memory_space=pltpu.HBM),
-        ),
+        in_specs=[vmem, hbm, hbm, hbm, hbm]
+        + [vmem] * 8
+        + [pl.BlockSpec(memory_space=pltpu.SMEM)],
+        out_specs=(vmem, vmem, vmem, hbm),
         scratch_shapes=buffers(RING, RING, 8, 16)
         + buffers(RING, RING, 2, 16)
         + buffers(2, RING, 4, 16)
@@ -680,27 +859,28 @@
             pltpu.VMEM((width, units), jnp.bfloat16),
             pltpu.VMEM((width, units), jnp.bfloat16),
             pltpu.VMEM((2, RING, RING, 2, 16, parts[0][1]), jnp.bfloat16),
-            pltpu.SemaphoreType.DMA((192,)),
-            pltpu.SemaphoreType.DMA((192,)),
+            pltpu.VMEM((2, 2, RING, RING, 2, 16, units), jnp.bfloat16),
+            floats(8, RING, RING, 1, LANES),
+            floats(RING, 8, RING, 1, LANES),
+            floats(RING, RING, 8, 1, LANES),
+            floats(experts, LANES),
+            pltpu.VMEM((tokens, experts), jnp.bfloat16),
+            floats(2, RING, RING, RING, 32, experts),
+            floats(RING, RING, RING, 32, experts),
+        ]
+        + [floats(3, RING, RING, band, experts) for band in bands]
+        + [floats(3, RING, band, experts) for band in bands]
+        + [floats(3, band, experts) for band in bands]
+        + [
+            pltpu.SemaphoreType.DMA((224,)),
+            pltpu.SemaphoreType.DMA((224,)),
             pltpu.SemaphoreType.DMA((16,)),
-            pltpu.SemaphoreType.DMA((8,)),
+            pltpu.SemaphoreType.DMA((12,)),
         ],
         compiler_params=pltpu.CompilerParams(
-            collective_id=1, has_side_effects=True, vmem_limit_bytes=63 * 2**20
+            collective_id=1, has_side_effects=True, vmem_limit_bytes=67043328
         ),
-    )(grad_first, grad_second, w_gate, w_up, tables)[0]
-
-
-def in_blocks(shard, dim, size):
-    shape = shard.shape
-    parts = shard.reshape(*shape[:dim], size, shape[dim] // size, *shape[dim + 1 :])
-    return jnp.moveaxis(parts, dim, 0)
-
-
-def summed_on_arrival(shard, axis, dim):
-    size = lax.axis_size(axis)
-    parts = lax.all_to_all(in_blocks(shard, dim, size), axis, 0, 0, tiled=True)
-    return jnp.sum(parts, axis=0)
+    )(values, *grads, *weights, tables, inputs, router, probs, gates, place, scale, ids, aux)[:3]
 
 
 def hidden_backward(upstream, pre_gate, pre_up):
@@ -730,9 +910,8 @@
     aux_weight,
 ):
     devices = lax.axis_size(AXES)
-    seq_size = lax.axis_size(SEQ)
     inputs, upstream_grad, chosen_ids = tokens[0], out_grad[0], expert_ids[0]
-    tok_rows, top_count = chosen_ids.shape
+    tok_rows = chosen_ids.shape[0]
     model_width = inputs.shape[1]
     experts = router_weight.shape[1]
     capacity = saved_gate.shape[1] // devices
@@ -754,11 +933,12 @@
     offset = (position - tok_rows).astype(jnp.float32)
     slot_token = jnp.sum(filled * offset[:, None, None], axis=0) + tok_rows
     slot_gate = jnp.sum(filled * gates[:, None, :], axis=0)
+    counts = jnp.pad(jnp.sum(mask, axis=0, keepdims=True), ((0, capacity - 1), (0, 0)))
     tables = []
     for a, b, s in ORDERS:
         both = jnp.stack([slot_token, slot_gate]).reshape(2, capacity, RING, RING, RING, 2)
         both = both.transpose(0, 2 + b, 2 + a, 2 + s, 5, 1)
-        tables.append(both.reshape(2 * RING * RING, LANES))
+        tables.append(jnp.concatenate([both.reshape(2 * RING * RING, LANES), counts]))
     tables = jnp.stack(tables).astype(jnp.bfloat16)
 
     _, seen, upstream = dispatch(parts, upstream_grad, tables, down_weight[0])
@@ -767,36 +947,24 @@
         saved_gate[0].reshape(upstream.shape),
         saved_up[0].reshape(upstream.shape),
     )
-    combine_back = lax.all_to_all(
-        slot_combine.reshape(1, devices, capacity), AXES, split_axis=1, concat_axis=0, tiled=True
-    ).reshape(experts, capacity)
-    expert_sum = combine(
-        parts, grad_first, grad_second, gate_weight[0], up_weight[0], seen, tok_rows
+    values = slot_combine.astype(jnp.float32).reshape(*upstream.shape[:4], 1, capacity)
+    values = jnp.pad(values, [(0, 0)] * 5 + [(0, LANES - capacity)])
+    token_grad, combine_grad, router_grad = combine(
+        parts,
+        values,
+        (grad_first, grad_second),
+        (gate_weight[0], up_weight[0]),
+        seen,
+        inputs,
+        router_weight,
+        probs,
+        gates,
+        jnp.where(mask > 0, slot_pos, -1.0),
+        chosen_sum,
+        chosen_ids,
+        aux_weight,
     )
-
-    in_seq = seen[0, :, :, : RING * RING].astype(jnp.float32)
-    used = jnp.sum((in_seq < tok_rows).astype(jnp.float32), axis=(0, 1))
-    used = jnp.sum(used.reshape(RING, RING, RING, 2, capacity), axis=-1)
-    seq_counts = used.transpose(1, 0, 2, 3).reshape(experts)
-
-    combine_dense = jnp.sum(filled * combine_back.T.astype(jnp.float32)[None], axis=1)
-    combine_grad = jnp.sum(
-        jnp.where(chosen_ids[:, :, None] == expert, combine_dense[:, None, :], 0.0), axis=-1
-    )
-    prob_sel = (
-        combine_dense - jnp.sum(gates * combine_dense, axis=1, keepdims=True)
-    ) / chosen_sum
-    fraction = experts * seq_counts / (top_count * tok_rows * seq_size)
-    prob_grad = prob_sel * mask + aux_weight[0] * fraction[None, :]
-    dlogits = probs * (prob_grad - jnp.sum(probs * prob_grad, axis=1, keepdims=True))
-    logit_grad = dlogits.astype(jnp.bfloat16)
-    token_grad = expert_sum + jnp.einsum(
-        "te,de->td", logit_grad, router_weight, preferred_element_type=jnp.float32
-    )
-    router = jnp.einsum("td,te->de", inputs, logit_grad, preferred_element_type=jnp.float32)
-    for axis in AXES:
-        router = summed_on_arrival(router, axis, 0)
-    return (token_grad.astype(jnp.bfloat16)[None], combine_grad[None], router)
+    return (token_grad[None], combine_grad[None], router_grad)
 
 
 def solution(mesh):

time: 384 us -> 334 us (0.87)
  blocking collectives: 32.2 us -> 0 us
  starting transfers between devices: 20.2 us -> 0 us
  Pallas kernels: 294 us -> 305 us
  waiting for transfers between devices: 4.98 us -> 0 us
    all_to_all x2 -> x0, blocking collectives: 32.2 us -> none  [summed_on_arrival(): parts = lax.all_to_all(in_blocks(shard, dim, size), axis, 0, 0, tiled=True)]
    all_to_all x3 -> x0, starting transfers between devices: 20.2 us -> none  [the longest x2 10.3 us: summed_on_arrival(): parts = lax.all_to_all(in_blocks(shard, dim, size), axis, 0, 0, tiled=True)]
    reduce_sum x12 -> x0, other arithmetic: 12.8 us -> none  [the longest x1 9.91 us: hidden_backward(): slot_combine = jnp.sum(upstream * hidden, axis=-1).astype(jnp.bfloat16)]
    pallas_call x1, Pallas kernels: 149 us -> 160 us  [combine(): pl.pallas_call(functools.partial(combine_kernel, parts), out_shape=(jax.S...]
    convert_element_type x2 -> x1, other arithmetic: 0.16 us -> 9.28 us  [hidden_backward(): (upstream * second * gate_sig * (1.0 + first * (1.0 - gate_sig))).astype(...]
    unnamed x4 -> x10, local copies, waits for them, and re-layouts: 0.87 us -> 6.66 us
    all_to_all x3 -> x0, waiting for transfers between devices: 4.98 us -> none  [the longest x1 2.74 us: shards(): lax.all_to_all(slot_combine.reshape(1, devices, capacity), AXES, split_ax...]
  transfers between devices with their start and end apart: 3 -> 0, of which waited for: 2 -> 0; matrix products, arithmetic and copies ran while one was open for 2% -> 0% of each run, Pallas kernels for 39% -> 0%
where the time goes in v1:
time: 334 us; the launch traced here: 330 us
  Pallas kernels  305 us (91%)
  other arithmetic  11.8 us (4%)
  local copies, waits for them, and re-layouts  8.25 us (2%)
    pallas_call x1, Pallas kernels, combine(): pl.pallas_call(functools.partial(combine_kernel, parts), out_shape=(jax.S...  160 us
    pallas_call x1, Pallas kernels, dispatch(): pl.pallas_call(functools.partial(dispatch_kernel, parts), out_shape=(jax....  146 us
    convert_element_type x1, other arithmetic, hidden_backward(): (upstream * second * gate_sig * (1.0 + first * (1.0 - gate_sig))).astype(...  9.28 us

profile of v1, /device:TPU:82, one launch (start us, length us, event | category | flops | bytes accessed | tf_op | source)
XLA Modules:
  0.0 329.9 jit_solution(13818473082925277836)
XLA Ops:
  0.6 0.0 copy-start
  1.4 0.9 copy.27
  2.4 0.0 copy-start.1
  2.4 0.2 convert_reduce_fusion.1
  2.6 2.1 fusion.23
  4.7 0.1 copy.29
  4.8 0.2 fusion.14
  5.0 0.8 fusion.21
  5.8 0.1 broadcast_divide_fusion.gates
  5.9 0.0 copy-start.2
  5.9 0.6 copy-done.2
  6.5 0.3 fusion.9
  6.9 0.1 copy.28
  7.0 0.1 copy.30
  7.1 0.1 fusion.26
  7.3 0.1 reshape.71
  7.4 0.1 fusion.25
  7.5 0.1 fusion.27
  7.7 0.1 reshape.70
  7.8 0.1 reshape.72
  8.0 0.6 pad_maximum_fusion.maps
  8.6 0.7 copy.35.scale
  9.3 145.6 %shard_map.121 = (bf16[4,4,4,2,16,4096]{5,4,3,2,1,0:T(8,128)(2,1)}, bf16[3,4,4,48,128]{4,3,2,1,0:T(8,128)(2,1)}, f32[4,4,4,2,16,768]{5,4,3,2,1,0:T(8,128)}) custom-call(bf16[128,4096]{1,0:T(8,128)(2,1)} %bitcast.42, bf16[3,48,128]{2,1,0:T(8,128)(2,1)} %pad_maximum_fusion.maps, bf16[768,4096]{1,0:T(8,128)(2,1)} %bitcast.36), custom_call_target="tpu_custom_call" | custom-call | tf_op jit(solution)/shard_map/pallas_call | solution.py:364
  154.9 0.0 copy-done
  154.9 9.3 %fusion.4 = (bf16[4,4,4,2,16,768]{5,4,3,2,1,0:T(8,128)(2,1)}, bf16[4,4,4,2,16]{4,3,2,1,0:T(2,128)(2,1)S(1)}, bf16[4,4,4,2,16,768]{5,4,3,2,1,0:T(8,128)(2,1)}) fusion(f32[4,4,4,2,16,768]{5,4,3,2,1,0:T(8,128)} %get-tuple-element.8, bf16[4,4,4,2,16,768]{5,4,3,2,1,0:T(8,128)(2,1)S(1)} %bitcast.40, bf16[4,4,4,2,16,768]{5,4,3,2,1,0:T(8,128)(2,1)} %bitcast.41), kind=kLoop, calls=%fused_computation.9 | loop fusion | flops 28309504 | bytes 18878464 | tf_op jit(solution)/shard_map/convert_element_type | solution.py:893
  164.2 0.0 copy-done.1
  164.2 0.1 copy.34
  164.3 0.7 pad_convert_fusion.values
  165.0 159.8 %shard_map.122 = (bf16[128,4096]{1,0:T(8,128)(2,1)}, f32[128,8]{1,0:T(8,128)}, f32[32,128]{1,0:T(8,128)}, bf16[4,4,4,2,16,4096]{5,4,3,2,1,0:T(8,128)(2,1)}) custom-call(f32[4,4,4,2,1,128]{5,4,3,2,1,0:T(1,128)} %pad_convert_fusion.values, bf16[4,4,4,2,16,768]{5,4,3,2,1,0:T(8,128)(2,1)} %get-tuple-element.31.grad_first, ...), custom_call_target="tpu_custom_call" | custom-call | tf_op jit(solution)/shard_map/pallas_call | solution.py:840
  324.7 1.5 copy.36
  326.2 2.3 copy.40
  328.5 1.3 copy.41
  (7 shorter events, 0.2 us)
Async XLA Ops:
  0.6 154.3 %copy-start = (bf16[1,2048,768]{2,1,0:T(8,128)(2,1)S(1)}, bf16[1,2048,768]{2,1,0:T(8,128)(2,1)}, u32[]{:S(2)}) copy-start(bf16[1,2048,768]{2,1,0:T(8,128)(2,1)} %param.17) | copy-start | bytes 9437188
  2.4 161.8 %copy-start.1 = (s32[1,128,8]{2,1,0:T(8,128)}, s32[1,128,8]{2,1,0:T(8,128)S(1)}, u32[]{:S(2)}) copy-start(s32[1,128,8]{2,1,0:T(8,128)S(1)} %copy.27) | copy-start | bytes 12292
  5.9 0.6 copy-start.2

commit v2 on v1

--- a/solution.py
+++ b/solution.py
@@ -15,6 +15,7 @@
 RING = 4
 LANES = 128
 ORDERS = ((0, 1, 2), (1, 2, 0), (2, 0, 1))
+STRIDES = (32, 8, 2)
 
 
 def column_parts(width):
@@ -86,12 +87,6 @@
     return ref.at[where[0], where[1], where[2], c_index, :, pl.ds(start, size)]
 
 
-def line_row(table, line):
-    rows = table.astype(jnp.float32)
-    index = lax.broadcasted_iota(jnp.int32, rows.shape, 0)
-    return jnp.sum(jnp.where(index == line, rows, 0.0), axis=0, keepdims=True)
-
-
 def fixed_b(order, b_index):
     where = [slice(None)] * 3
     where[order[1]] = b_index
@@ -99,8 +94,10 @@
 
 
 def dispatch_kernel(
-    parts, grad, maps, down, slots, maps_out, upstream,
-    g0, g1, g2, o0, o1, o2, l0, l1, l2, seen, weight, batch, ss, rs, ls, bs,
+    parts, grad, inputs, router, ids, down,
+    slots, upstream, lines, counts, probs, gates, place, scale,
+    g0, g1, g2, o0, o1, o2, l0, l1, l2, seen, picks, tokens_in, router_in, weight, batch,
+    ss, rs, ls, bs,
 ):
     held, outgoing, relay = (g0, g1, g2), (o0, o1, o2), (l0, l1, l2)
     here = Place()
@@ -117,9 +114,12 @@
     for p, (a, b, s) in enumerate(ORDERS):
         start, size = parts[p]
         keep(grad.at[:, pl.ds(start, size)], held[p].at[here.at[b], here.at[a]])
-        keep(maps.at[p], seen.at[p, here.at[b], here.at[a]])
-    fetch = pltpu.make_async_copy(down, weight, bs.at[2])
-    fetch.start()
+    fetches = [
+        pltpu.make_async_copy(src, dst, bs.at[2 + n])
+        for n, (src, dst) in enumerate(((inputs, tokens_in), (router, router_in), (down, weight)))
+    ]
+    for copy in fetches:
+        copy.start()
     here.greet()
     for copy in local:
         copy.wait()
@@ -144,13 +144,52 @@
             piece = held[p].at[here.along(b, 2), here.along(a, step), rows]
             wires.arrived(piece, (p, "m2far", way, k), here.near(b, -way))
 
-    for p, (a, b, s) in enumerate(ORDERS):
-        table = seen.at[p, here.at[b], here.at[a]]
+    def route():
+        experts = router.shape[1]
+        row = lax.broadcasted_iota(jnp.int32, (tokens, experts), 0)
+        lane = lax.broadcasted_iota(jnp.int32, (tokens, experts), 1)
+        mask = jnp.zeros((tokens, experts), jnp.float32)
+        for k in range(ids.shape[1]):
+            mask = mask + jnp.where(lane == ids[:, k : k + 1], 1.0, 0.0)
+        before = jnp.where(row > lane, 1.0, 0.0).astype(jnp.bfloat16)
+        rank = jnp.dot(before, mask.astype(jnp.bfloat16), preferred_element_type=jnp.float32)
+        place[...] = jnp.where(mask > 0, rank, -1.0)
+        logits = jnp.dot(tokens_in[...], router_in[...], preferred_element_type=jnp.float32)
+        powers = jnp.exp(logits - jnp.max(logits, axis=1, keepdims=True))
+        probs[...] = powers / jnp.sum(powers, axis=1, keepdims=True)
+        chosen = probs[...] * mask
+        scale[...] = jnp.sum(chosen, axis=1, keepdims=True)
+        gates[...] = chosen / scale[...]
+        slot = lax.broadcasted_iota(jnp.int32, (16, experts), 0)
+        token_of = jnp.zeros((16, experts), jnp.float32)
+        gate_of = jnp.zeros((16, experts), jnp.float32)
+        offset = (row - tokens).astype(jnp.float32)
+        for j in range(16):
+            hit = place[...] == j
+            token = jnp.sum(jnp.where(hit, offset, 0.0), axis=0, keepdims=True) + tokens
+            gate = jnp.sum(jnp.where(hit, gates[...], 0.0), axis=0, keepdims=True)
+            token_of = jnp.where(slot == j, token, token_of)
+            gate_of = jnp.where(slot == j, gate, gate_of)
+        count = jnp.where(slot == 0, jnp.sum(mask, axis=0, keepdims=True), 0.0)
+        for p, (a, b, s) in enumerate(ORDERS):
+            for n, part in enumerate((token_of, gate_of, count)):
+                seen[p, here.at[b], here.at[a], pl.ds(16 * n, 16), :] = part.astype(jnp.bfloat16)
+        for p, (a, b, s) in enumerate(ORDERS):
+            first = here.at[a] * STRIDES[a] + here.at[b] * STRIDES[b]
+            expert = first + lane // 32 * STRIDES[s] + lane // 16 % 2
+            picks[p] = jnp.where(row == expert, 1.0, 0.0).astype(jnp.bfloat16)
+
+    for p, (a, b, s) in enumerate(ORDERS):
         block = held[p].at[here.at[b], here.at[a]]
         for way in (1, -1):
+            wires.send(block, block, here.near(a, way), (p, "m1", way))
+    for copy in fetches[:2]:
+        copy.wait()
+    route()
+    for p, (a, b, s) in enumerate(ORDERS):
+        table = seen.at[p, here.at[b], here.at[a]]
+        for way in (1, -1):
             wires.send(table, table, here.near(a, way), (p, "t1", way))
-        for way in (1, -1):
-            wires.send(block, block, here.near(a, way), (p, "m1", way))
     for p in range(3):
         pass_on(p, 0, 0)
     for p, (a, b, s) in enumerate(ORDERS):
@@ -190,11 +229,21 @@
     def select(p, k, b_step):
         a, b, s = ORDERS[p]
         b_index = here.along(b, b_step)
-        line = here.at[b] * RING + here.at[a]
         size = parts[p][1]
+        found = jnp.dot(
+            seen[p, b_index].reshape(RING * 48, LANES),
+            picks[p],
+            preferred_element_type=jnp.float32,
+        ).reshape(RING, 3, 16, LANES)
+        slot = lax.broadcasted_iota(jnp.int32, found.shape, 2)
+        lane = lax.broadcasted_iota(jnp.int32, found.shape, 3)
+        found = jnp.sum(jnp.where(slot == lane % 16, found, 0.0), axis=2)
+        for a_index in range(RING):
+            for n in range(2):
+                lines[p, b_index, a_index, pl.ds(n, 1), :] = found[a_index, n : n + 1]
 
         def one(a_index, carry):
-            token_of = line_row(seen[p, b_index, a_index, pl.ds(0, 16), :], line)
+            token_of = lines[p, b_index, a_index, pl.ds(0, 1), :]
             token = lax.broadcasted_iota(jnp.int32, (tokens, LANES), 0).astype(jnp.float32)
             pick = jnp.where(token == token_of, 1.0, 0.0).astype(jnp.bfloat16)
             rows = lax.dot_general(
@@ -289,7 +338,7 @@
 
     def ready(p, k):
         received(p, k, turns[k])
-        local[6 + k * 3 + p].wait()
+        local[3 + k * 3 + p].wait()
         batch_copy(p, k).start()
 
     def project(p, k):
@@ -336,9 +385,10 @@
     for p in range(3):
         select(p, 3, 2)
         deliver(p, 3, 2)
-    maps_out[...] = seen[...]
+    total = jnp.sum(seen[0, :, :, pl.ds(32, 16), :].astype(jnp.float32), axis=(0, 1))
+    counts[...] = jnp.sum(total, axis=0, keepdims=True)
     upstream[...] = jnp.zeros_like(upstream)
-    fetch.wait()
+    fetches[2].wait()
     for p in range(3):
         forward(p, 1, turns[1])
     work = [(k, p) for k in range(4) for p in range(3)]
@@ -354,46 +404,51 @@
     wires.drain()
 
 
-def dispatch(parts, grad, maps, down):
+def dispatch(parts, grad, inputs, router, ids, down):
     tokens, width = grad.shape
+    units, experts = down.shape[0], router.shape[1]
     rows = [pltpu.VMEM((RING, RING, tokens, size), jnp.bfloat16) for _, size in parts]
     outs = [pltpu.VMEM((RING, 8, RING, 16, size), jnp.bfloat16) for _, size in parts]
     relays = [pltpu.VMEM((RING, 2, RING, 16, size), jnp.bfloat16) for _, size in parts]
-    table = (3, RING, RING, maps.shape[1], LANES)
-    units = down.shape[0]
+    hbm, vmem = pl.BlockSpec(memory_space=pltpu.HBM), pl.BlockSpec(memory_space=pltpu.VMEM)
+    square = jax.ShapeDtypeStruct((tokens, experts), jnp.float32)
     return pl.pallas_call(
         functools.partial(dispatch_kernel, parts),
         out_shape=(
             jax.ShapeDtypeStruct((RING, RING, RING, 2, 16, width), jnp.bfloat16),
-            jax.ShapeDtypeStruct(table, jnp.bfloat16),
             jax.ShapeDtypeStruct((RING, RING, RING, 2, 16, units), jnp.float32),
+            jax.ShapeDtypeStruct((3, RING, RING, 8, LANES), jnp.float32),
+            jax.ShapeDtypeStruct((1, experts), jnp.float32),
+            square,
+            square,
+            square,
+            jax.ShapeDtypeStruct((tokens, 1), jnp.float32),
         ),
-        in_specs=[pl.BlockSpec(memory_space=pltpu.HBM)] * 3,
-        out_specs=(
-            pl.BlockSpec(memory_space=pltpu.HBM),
-            pl.BlockSpec(memory_space=pltpu.VMEM),
-            pl.BlockSpec(memory_space=pltpu.VMEM),
-        ),
+        in_specs=[hbm, hbm, hbm, vmem, hbm],
+        out_specs=(hbm,) + (vmem,) * 7,
         scratch_shapes=rows
         + outs
         + relays
         + [
-            pltpu.VMEM(table, jnp.bfloat16),
+            pltpu.VMEM((3, RING, RING, 48, LANES), jnp.bfloat16),
+            pltpu.VMEM((3, experts, LANES), jnp.bfloat16),
+            pltpu.VMEM((tokens, width), jnp.bfloat16),
+            pltpu.VMEM((width, experts), jnp.bfloat16),
             pltpu.VMEM((units, width), jnp.bfloat16),
             pltpu.VMEM((2, RING, RING, 2, 16, parts[0][1]), jnp.bfloat16),
             pltpu.SemaphoreType.DMA((192,)),
             pltpu.SemaphoreType.DMA((192,)),
             pltpu.SemaphoreType.DMA((32,)),
-            pltpu.SemaphoreType.DMA((3,)),
+            pltpu.SemaphoreType.DMA((5,)),
         ],
         compiler_params=pltpu.CompilerParams(
-            collective_id=0, has_side_effects=True, vmem_limit_bytes=60 * 2**20
+            collective_id=0, has_side_effects=True, vmem_limit_bytes=62 * 2**20
         ),
-    )(grad, maps, down)
+    )(grad, inputs, router, ids, down)[1:]
 
 
 def combine_kernel(
-    parts, values, grad_first, grad_second, w_gate, w_up, tables, inputs, router,
+    parts, values, grad_first, grad_second, w_gate, w_up, lines, counts, inputs, router,
     probs, gates, place, scale, ids, aux,
     out, combine_grad, router_grad, back,
     q0, q1, q2, l0, l1, l2, x0, x1, x2, y0, y1, y2, u0, u1, u2, v0, v1, v2,
@@ -499,10 +554,8 @@
         combine_grad[...] = picked
         inner = jnp.sum(gates[...] * dense, axis=1, keepdims=True)
         prob_grad = jnp.where(place[...] >= 0, (dense - inner) / scale[...], 0.0)
-        counts = jnp.sum(tables[0, :, :, pl.ds(32, 16), :].astype(jnp.float32), axis=(0, 1))
-        counts = jnp.sum(counts, axis=0, keepdims=True)
         top = combine_grad.shape[1]
-        fraction = dense.shape[1] * counts / (top * tokens * RING * RING)
+        fraction = dense.shape[1] * counts[...] / (top * tokens * RING * RING)
         prob_grad = prob_grad + aux[0] * fraction
         mean = jnp.sum(probs[...] * prob_grad, axis=1, keepdims=True)
         logit_grad[...] = (probs[...] * (prob_grad - mean)).astype(jnp.bfloat16)
@@ -685,12 +738,11 @@
     def add_up(p, b_step):
         a, b, s = ORDERS[p]
         b_index = here.along(b, b_step)
-        line = here.at[b] * RING + here.at[a]
         size = parts[p][1]
 
         def one(a_index, carry):
-            token_of = line_row(tables[p, b_index, a_index, pl.ds(0, 16), :], line)
-            gate_of = line_row(tables[p, b_index, a_index, pl.ds(16, 16), :], line)
+            token_of = lines[p, b_index, a_index, pl.ds(0, 1), :]
+            gate_of = lines[p, b_index, a_index, pl.ds(1, 1), :]
             token = lax.broadcasted_iota(jnp.int32, (tokens, LANES), 0).astype(jnp.float32)
             weigh = jnp.where(token == token_of, gate_of, 0.0).astype(jnp.bfloat16)
             total = jnp.dot(
@@ -709,27 +761,21 @@
             total = total + term.astype(jnp.float32)
         return total
 
-    def fold2(p, way):
+    def fold2(p, way, k, step):
         a, b, s = ORDERS[p]
-        b_index = here.along(b, way)
+        b_index, a_index = here.along(b, way), here.along(a, step)
         slot = 0 if way == 1 else 1
         groups = pl.ds(0, 4) if way == 1 else pl.ds(4, 4)
-        wires.arrived(halves2[p].at[slot], (p, "half2", way), here.near(b, -way))
-
-        def one(a_index, carry):
-            rows[p][b_index, a_index, groups] = plus(
-                rows[p][b_index, a_index, groups], halves2[p][slot, a_index]
-            ).astype(jnp.bfloat16)
-            return carry
-
-        lax.fori_loop(0, RING, one, 0)
-        for k, step in enumerate((2, 1, -1, 0)):
-            wires.send(
-                rows[p].at[b_index, here.along(a, step)],
-                whole2[p].at[slot, k],
-                here.near(b, way),
-                (p, "whole2", way, k),
-            )
+        wires.arrived(halves2[p].at[slot, k], (p, "half2", way, k), here.near(b, -way))
+        rows[p][b_index, a_index, groups] = plus(
+            rows[p][b_index, a_index, groups], halves2[p][slot, k]
+        ).astype(jnp.bfloat16)
+        wires.send(
+            rows[p].at[b_index, a_index],
+            whole2[p].at[slot, k],
+            here.near(b, way),
+            (p, "whole2", way, k),
+        )
 
     def settle2(p, k, step):
         a, b, s = ORDERS[p]
@@ -766,25 +812,28 @@
         gathered(p, 0, 2)
         add_up(p, 2)
         far = here.along(b, 2)
-        for way, groups in ((1, pl.ds(0, 4)), (-1, pl.ds(4, 4))):
-            wires.send(
-                rows[p].at[far, :, groups],
-                halves2[p].at[0 if way == 1 else 1],
-                here.near(b, way),
-                (p, "half2", way),
-            )
+        for k, step in enumerate(order):
+            for way, groups in ((1, pl.ds(0, 4)), (-1, pl.ds(4, 4))):
+                wires.send(
+                    rows[p].at[far, here.along(a, step), groups],
+                    halves2[p].at[0 if way == 1 else 1, k],
+                    here.near(b, way),
+                    (p, "half2", way, k),
+                )
     for q in range(3):
         forward(q, 3, order[3])
-    for k, way in ((1, 1), (2, -1)):
+    for k in (1, 2, 3):
         for p in range(3):
-            gathered(p, k, way)
-            add_up(p, way)
-            fold2(p, way)
-        sum_in(k - 1)
-        sum_send(k)
-    for p in range(3):
-        gathered(p, 3, 0)
-        add_up(p, 0)
+            gathered(p, k, order[k])
+            add_up(p, order[k])
+    sum_in(0)
+    sum_send(1)
+    for k, step in enumerate(order):
+        for way in (1, -1):
+            for p in range(3):
+                fold2(p, way, k, step)
+    sum_in(1)
+    sum_send(2)
     for p, (a, b, s) in enumerate(ORDERS):
         block = rows[p].at[here.at[b], here.along(a, 2)]
         block[...] = settle2(p, 0, 2).astype(jnp.bfloat16)
@@ -824,7 +873,7 @@
     wires.drain()
 
 
-def combine(parts, values, grads, weights, tables, inputs, router, probs, gates, place, scale, ids, aux):
+def combine(parts, values, grads, weights, lines, counts, inputs, router, probs, gates, place, scale, ids, aux):
     width, units = weights[0].shape
     tokens, top = ids.shape
     experts = probs.shape[1]
@@ -846,7 +895,7 @@
             jax.ShapeDtypeStruct((RING, RING, RING, 2, 16, width), jnp.bfloat16),
         ),
         in_specs=[vmem, hbm, hbm, hbm, hbm]
-        + [vmem] * 8
+        + [vmem] * 9
         + [pl.BlockSpec(memory_space=pltpu.SMEM)],
         out_specs=(vmem, vmem, vmem, hbm),
         scratch_shapes=buffers(RING, RING, 8, 16)
@@ -880,7 +929,7 @@
         compiler_params=pltpu.CompilerParams(
             collective_id=1, has_side_effects=True, vmem_limit_bytes=67043328
         ),
-    )(values, *grads, *weights, tables, inputs, router, probs, gates, place, scale, ids, aux)[:3]
+    )(values, *grads, *weights, lines, counts, inputs, router, probs, gates, place, scale, ids, aux)[:3]
 
 
 def hidden_backward(upstream, pre_gate, pre_up):
@@ -911,37 +960,13 @@
 ):
     devices = lax.axis_size(AXES)
     inputs, upstream_grad, chosen_ids = tokens[0], out_grad[0], expert_ids[0]
-    tok_rows = chosen_ids.shape[0]
     model_width = inputs.shape[1]
-    experts = router_weight.shape[1]
     capacity = saved_gate.shape[1] // devices
     parts = column_parts(model_width)
 
-    logits = jnp.dot(inputs, router_weight, preferred_element_type=jnp.float32)
-    probs = jax.nn.softmax(logits, axis=-1)
-    expert = jnp.arange(experts, dtype=jnp.int32)
-    mask = jnp.sum((chosen_ids[:, :, None] == expert).astype(jnp.float32), axis=1)
-    chosen_sum = jnp.sum(probs * mask, axis=1, keepdims=True)
-    gates = probs * mask / chosen_sum
-    position = jnp.arange(tok_rows)
-    before = (position[:, None] > position[None, :]).astype(jnp.bfloat16)
-    slot_pos = jnp.dot(before, mask.astype(jnp.bfloat16), preferred_element_type=jnp.float32)
-    slot = jnp.arange(capacity, dtype=jnp.float32)
-    filled = jnp.where(
-        (slot_pos[:, None, :] == slot[None, :, None]) & (mask[:, None, :] > 0), 1.0, 0.0
+    upstream, lines, counts, probs, gates, place, chosen_sum = dispatch(
+        parts, upstream_grad, inputs, router_weight, chosen_ids, down_weight[0]
     )
-    offset = (position - tok_rows).astype(jnp.float32)
-    slot_token = jnp.sum(filled * offset[:, None, None], axis=0) + tok_rows
-    slot_gate = jnp.sum(filled * gates[:, None, :], axis=0)
-    counts = jnp.pad(jnp.sum(mask, axis=0, keepdims=True), ((0, capacity - 1), (0, 0)))
-    tables = []
-    for a, b, s in ORDERS:
-        both = jnp.stack([slot_token, slot_gate]).reshape(2, capacity, RING, RING, RING, 2)
-        both = both.transpose(0, 2 + b, 2 + a, 2 + s, 5, 1)
-        tables.append(jnp.concatenate([both.reshape(2 * RING * RING, LANES), counts]))
-    tables = jnp.stack(tables).astype(jnp.bfloat16)
-
-    _, seen, upstream = dispatch(parts, upstream_grad, tables, down_weight[0])
     grad_first, grad_second, slot_combine = hidden_backward(
         upstream,
         saved_gate[0].reshape(upstream.shape),
@@ -954,12 +979,13 @@
         values,
         (grad_first, grad_second),
         (gate_weight[0], up_weight[0]),
-        seen,
+        lines,
+        counts,
         inputs,
         router_weight,
         probs,
         gates,
-        jnp.where(mask > 0, slot_pos, -1.0),
+        place,
         chosen_sum,
         chosen_ids,
         aux_weight,

time: 334 us -> 338 us (1.012)
  Pallas kernels: 305 us -> 314 us
    pallas_call x1, Pallas kernels: 160 us -> 168 us  [combine(): pl.pallas_call(functools.partial(combine_kernel, parts), out_shape=(jax.S...]
where the time goes in v2:
time: 338 us; the launch traced here: 333 us
  Pallas kernels  314 us (93%)
  other arithmetic  10.5 us (3%)
  local copies, waits for them, and re-layouts  6.58 us (2%)
    pallas_call x1, Pallas kernels, combine(): pl.pallas_call(functools.partial(combine_kernel, parts), out_shape=(jax.S...  168 us
    pallas_call x1, Pallas kernels, dispatch(): pl.pallas_call(functools.partial(dispatch_kernel, parts), out_shape=(jax....  146 us
    convert_element_type x1, other arithmetic, hidden_backward(): (upstream * second * gate_sig * (1.0 + first * (1.0 - gate_sig))).astype(...  9.76 us

profile of v2, /device:TPU:82, one launch (start us, length us, event | category | flops | bytes accessed | tf_op | source)
XLA Modules:
  0.0 332.5 jit_solution(17022619883237707685)
XLA Ops:
  1.3 1.4 copy.15
  2.7 146.1 %shard_map.121 = (bf16[4,4,4,2,16,4096]{5,4,3,2,1,0:T(8,128)(2,1)}, f32[4,4,4,2,16,768]{5,4,3,2,1,0:T(8,128)}, f32[3,4,4,8,128]{4,3,2,1,0:T(8,128)}, f32[1,128]{...) custom-call(bf16[128,4096]{1,0:T(8,128)(2,1)} %bitcast.22, ...), custom_call_target="tpu_custom_call" | custom-call | tf_op jit(solution)/shard_map/pallas_call | solution.py:415
  148.8 9.8 %fusion.4 = (bf16[4,4,4,2,16,768]{5,4,3,2,1,0:T(8,128)(2,1)}, bf16[4,4,4,2,16]{4,3,2,1,0:T(2,128)(2,1)S(1)}, bf16[4,4,4,2,16,768]{5,4,3,2,1,0:T(8,128)(2,1)}) fusion(f32[4,4,4,2,16,768]{5,4,3,2,1,0:T(8,128)} %get-tuple-element.13, bf16[4,4,4,2,16,768]{5,4,3,2,1,0:T(8,128)(2,1)} %bitcast.20, bf16[4,4,4,2,16,768]{5,4,3,2,1,0:T(8,128)(2,1)} %bitcast.21), kind=kLoop, calls=%fused_computation.9 | loop fusion | flops 28309504 | bytes 18878464 | tf_op jit(solution)/shard_map/convert_element_type | solution.py:942
  158.5 0.1 copy.16
  158.6 0.7 pad_convert_fusion.values
  159.3 168.1 %shard_map.122 = (bf16[128,4096]{1,0:T(8,128)(2,1)}, f32[128,8]{1,0:T(8,128)}, f32[32,128]{1,0:T(8,128)}, bf16[4,4,4,2,16,4096]{5,4,3,2,1,0:T(8,128)(2,1)}) custom-call(f32[4,4,4,2,1,128]{5,4,3,2,1,0:T(1,128)} %pad_convert_fusion.values, bf16[4,4,4,2,16,768]{5,4,3,2,1,0:T(8,128)(2,1)} %get-tuple-element.29.grad_first, ...), custom_call_target="tpu_custom_call" | custom-call | tf_op jit(solution)/shard_map/pallas_call | solution.py:889
  327.4 1.5 copy.17
  328.9 2.3 copy.21
  331.2 1.3 copy.22

commit v3 on v2

--- a/solution.py
+++ b/solution.py
@@ -16,6 +16,21 @@
 LANES = 128
 ORDERS = ((0, 1, 2), (1, 2, 0), (2, 0, 1))
 STRIDES = (32, 8, 2)
+DISPATCH_PLAN = (
+    ("relay", 0), ("choose", 0), ("relay", 1), ("relay", 2), ("relay", 3), ("choose", 1), ("pass", 0),
+    ("choose", 2), ("far",), ("pass", 1), ("choose", 3), ("clear",),
+    ("near", 0), ("pass", 2), ("near", 1), ("distant", 0), ("pass", 3), ("near", 2),
+    ("distant", 1), ("near", 3), ("distant", 2), ("distant", 3),
+)
+COMBINE_PLAN = (
+    ("line",), ("make", 0), ("post", 0), ("make", 1), ("post", 1), ("make", 2), ("post", 2), ("x",),
+    ("make", 3), ("post", 3), ("make", 4), ("post", 4), ("pass", 0), ("make", 5), ("post", 5), ("z",),
+    ("make", 6), ("post", 6), ("make", 7), ("post", 7), ("pass", 1), ("make", 8), ("post", 8),
+    ("total", 0), ("halve",), ("router",), ("make", 9), ("post", 9), ("pass", 2), ("make", 10), ("post", 10),
+    ("make", 11), ("post", 11), ("chip",), ("send", 0), ("pass", 3),
+    ("total", 1), ("fold", 1), ("in", 0), ("send", 1),
+    ("total", 2), ("fold", -1), ("in", 1), ("send", 2), ("total", 3),
+)
 
 
 def column_parts(width):
@@ -96,7 +111,7 @@
 def dispatch_kernel(
     parts, grad, inputs, router, ids, down,
     slots, upstream, lines, counts, probs, gates, place, scale,
-    g0, g1, g2, o0, o1, o2, l0, l1, l2, seen, picks, tokens_in, router_in, weight, batch,
+    g0, g1, g2, o0, o1, o2, l0, l1, l2, seen, picks, tokens_in, router_in, weight, batch, last,
     ss, rs, ls, bs,
 ):
     held, outgoing, relay = (g0, g1, g2), (o0, o1, o2), (l0, l1, l2)
@@ -115,7 +130,7 @@
         start, size = parts[p]
         keep(grad.at[:, pl.ds(start, size)], held[p].at[here.at[b], here.at[a]])
     fetches = [
-        pltpu.make_async_copy(src, dst, bs.at[2 + n])
+        pltpu.make_async_copy(src, dst, bs.at[8 + n])
         for n, (src, dst) in enumerate(((inputs, tokens_in), (router, router_in), (down, weight)))
     ]
     for copy in fetches:
@@ -149,8 +164,9 @@
         row = lax.broadcasted_iota(jnp.int32, (tokens, experts), 0)
         lane = lax.broadcasted_iota(jnp.int32, (tokens, experts), 1)
         mask = jnp.zeros((tokens, experts), jnp.float32)
-        for k in range(ids.shape[1]):
-            mask = mask + jnp.where(lane == ids[:, k : k + 1], 1.0, 0.0)
+        by_token = ids[...].T
+        for k in range(ids.shape[0]):
+            mask = mask + jnp.where(lane == by_token[:, k : k + 1], 1.0, 0.0)
         before = jnp.where(row > lane, 1.0, 0.0).astype(jnp.bfloat16)
         rank = jnp.dot(before, mask.astype(jnp.bfloat16), preferred_element_type=jnp.float32)
         place[...] = jnp.where(mask > 0, rank, -1.0)
@@ -301,12 +317,11 @@
                 relay[p].at[k, core], theirs, here.near(s, way, other), (p, "far", other, k)
             )
 
-    def received(p, k, b_step):
+    def near_in(p, k):
         order = ORDERS[p]
         a, b, s = order
         start, size = parts[p]
-        b_index = here.along(b, b_step)
-        way = 1 if k % 2 == 0 else -1
+        b_index = here.along(b, turns[k])
         for other in (0, 1):
             core = 1 - here.core if other else here.core
             for step in (1, -1):
@@ -315,92 +330,121 @@
                     (p, "near", step, other, k),
                     here.near(s, -step, other),
                 )
+        wires.arrived(
+            slots_of(slots, order, b_index, here.at[s], 1 - here.core, start, size),
+            (p, "chip", k),
+            here.partner(),
+        )
+        local[3 + k * 3 + p].wait()
+
+    def distant_in(p, k):
+        order = ORDERS[p]
+        a, b, s = order
+        start, size = parts[p]
+        b_index = here.along(b, turns[k])
+        way = 1 if k % 2 == 0 else -1
+        for other in (0, 1):
+            core = 1 - here.core if other else here.core
             wires.arrived(
                 slots_of(slots, order, b_index, here.along(s, 2), core, start, size),
                 (p, "far", other, k),
                 here.near(s, -way, other),
             )
-        wires.arrived(
-            slots_of(slots, order, b_index, here.at[s], 1 - here.core, start, size),
-            (p, "chip", k),
-            here.partner(),
-        )
-
-    def batch_copy(p, k):
+
+    def copies(p, k, senders):
+        order = ORDERS[p]
         start, size = parts[p]
-        b_index = here.along(ORDERS[p][1], turns[k])
+        b_index = here.along(order[1], turns[k])
         slot = (k * 3 + p) % 2
-        return pltpu.make_async_copy(
-            slots.at[(*fixed_b(ORDERS[p], b_index), slice(None), slice(None), pl.ds(start, size))],
-            batch.at[slot, :, :, :, :, pl.ds(0, size)],
-            bs.at[slot],
-        )
-
-    def ready(p, k):
-        received(p, k, turns[k])
-        local[3 + k * 3 + p].wait()
-        batch_copy(p, k).start()
-
-    def project(p, k):
+        target, first = (batch, 3 * slot) if len(senders) == 3 else (last, 6 + slot)
+        return [
+            pltpu.make_async_copy(
+                slots_of(
+                    slots, order, b_index, here.along(order[2], step), slice(None), start, size
+                ),
+                target.at[slot, n, :, :, :, pl.ds(0, size)],
+                bs.at[first + n],
+            )
+            for n, step in enumerate(senders)
+        ]
+
+    def project(p, k, senders):
+        a, b, s = ORDERS[p]
         start, size = parts[p]
-        b_index = here.along(ORDERS[p][1], turns[k])
+        b_index = here.along(b, turns[k])
         slot = (k * 3 + p) % 2
-        batch_copy(p, k).wait()
-        where = fixed_b(ORDERS[p], b_index)
+        source = batch if len(senders) == 3 else last
+        for copy in copies(p, k, senders):
+            copy.wait()
 
         def tile(n, carry):
             units = pl.ds(pl.multiple_of(n * 256, 256), 256)
             term = lax.dot_general(
-                batch[slot, :, :, :, :, pl.ds(0, size)].reshape(512, size),
+                source[slot, :, :, :, :, pl.ds(0, size)].reshape(len(senders) * LANES, size),
                 weight[units, pl.ds(start, size)],
                 (((1,), (1,)), ((), ())),
                 preferred_element_type=jnp.float32,
-            )
-            there = (*where, slice(None), slice(None), units)
-            upstream[there] = upstream[there] + term.reshape(RING, RING, 2, 16, 256)
+            ).reshape(len(senders), RING, 2, 16, 256)
+            for m, step in enumerate(senders):
+                where = [slice(None)] * 3
+                where[b], where[s] = b_index, here.along(s, step)
+                there = (*where, slice(None), slice(None), units)
+                upstream[there] = upstream[there] + term[m]
             return carry
 
         lax.fori_loop(0, 3, tile, 0)
 
     turns = (0, -1, 1, 2)
-    for p in range(3):
-        relay_on(p, 0, 0)
-    for p in range(3):
-        select(p, 0, 0)
-        deliver(p, 0, 0)
-    for k, step in ((1, -1), (2, 1), (3, 2)):
+    joined = (0, -1, 1, 2)
+
+    def relays(k):
         for p in range(3):
-            relay_on(p, k, step)
-    for k in (1, 2):
+            relay_on(p, k, joined[k])
+
+    def choose(k):
         for p in range(3):
             select(p, k, turns[k])
             deliver(p, k, turns[k])
-    for p in range(3):
-        forward(p, 0, 0)
-    for p in range(3):
-        for k, step in ((0, 0), (1, -1), (2, 1), (3, 2)):
-            far_in(p, k, step)
-    for p, (a, b, s) in enumerate(ORDERS):
-        wires.arrived(seen.at[p, here.along(b, 2)], (p, "t2far"), here.near(b, -1))
-    for p in range(3):
-        select(p, 3, 2)
-        deliver(p, 3, 2)
-    total = jnp.sum(seen[0, :, :, pl.ds(32, 16), :].astype(jnp.float32), axis=(0, 1))
-    counts[...] = jnp.sum(total, axis=0, keepdims=True)
-    upstream[...] = jnp.zeros_like(upstream)
-    fetches[2].wait()
-    for p in range(3):
-        forward(p, 1, turns[1])
-    work = [(k, p) for k in range(4) for p in range(3)]
-    ready(work[0][1], work[0][0])
-    for turn, (k, p) in enumerate(work):
-        if turn + 1 < len(work):
-            after_k, after_p = work[turn + 1]
-            if after_p == 0 and after_k < 3:
-                for q in range(3):
-                    forward(q, after_k + 1, turns[after_k + 1])
-            ready(after_p, after_k)
-        project(p, k)
+
+    def far_rows():
+        for p, (a, b, s) in enumerate(ORDERS):
+            for k in range(RING):
+                far_in(p, k, joined[k])
+            wires.arrived(seen.at[p, here.along(b, 2)], (p, "t2far"), here.near(b, -1))
+
+    def pass_far(k):
+        for p in range(3):
+            forward(p, k, turns[k])
+
+    def clear():
+        total = jnp.sum(seen[0, :, :, pl.ds(32, 16), :].astype(jnp.float32), axis=(0, 1))
+        counts[...] = jnp.sum(total, axis=0, keepdims=True)
+        upstream[...] = jnp.zeros_like(upstream)
+        fetches[2].wait()
+
+    def multiply(k, arrive, senders):
+        def fetch(p):
+            arrive(p, k)
+            for copy in copies(p, k, senders):
+                copy.start()
+
+        fetch(0)
+        for p in range(3):
+            if p < 2:
+                fetch(p + 1)
+            project(p, k, senders)
+
+    actions = {
+        "relay": relays,
+        "choose": choose,
+        "far": far_rows,
+        "pass": pass_far,
+        "clear": clear,
+        "near": lambda k: multiply(k, near_in, (0, 1, -1)),
+        "distant": lambda k: multiply(k, distant_in, (2,)),
+    }
+    for name, *given_to in DISPATCH_PLAN:
+        actions[name](*given_to)
     wires.drain()
 
 
@@ -435,11 +479,12 @@
             pltpu.VMEM((tokens, width), jnp.bfloat16),
             pltpu.VMEM((width, experts), jnp.bfloat16),
             pltpu.VMEM((units, width), jnp.bfloat16),
-            pltpu.VMEM((2, RING, RING, 2, 16, parts[0][1]), jnp.bfloat16),
+            pltpu.VMEM((2, 3, RING, 2, 16, parts[0][1]), jnp.bfloat16),
+            pltpu.VMEM((2, 1, RING, 2, 16, parts[0][1]), jnp.bfloat16),
             pltpu.SemaphoreType.DMA((192,)),
             pltpu.SemaphoreType.DMA((192,)),
             pltpu.SemaphoreType.DMA((32,)),
-            pltpu.SemaphoreType.DMA((5,)),
+            pltpu.SemaphoreType.DMA((11,)),
         ],
         compiler_params=pltpu.CompilerParams(
             collective_id=0, has_side_effects=True, vmem_limit_bytes=62 * 2**20
@@ -544,17 +589,17 @@
         for j in range(16):
             dense = dense + jnp.where(place[...] == j, by_slot[j : j + 1], 0.0)
         lane = lax.broadcasted_iota(jnp.int32, dense.shape, 1)
-        column = lax.broadcasted_iota(jnp.int32, combine_grad.shape, 1)
-        picked = jnp.zeros(combine_grad.shape, jnp.float32)
-        for k in range(combine_grad.shape[1]):
+        by_token = ids[...].T
+        picked = jnp.zeros_like(dense)
+        for k in range(ids.shape[0]):
             value = jnp.sum(
-                jnp.where(lane == ids[:, k : k + 1], dense, 0.0), axis=1, keepdims=True
-            )
-            picked = picked + jnp.where(column == k, value, 0.0)
-        combine_grad[...] = picked
+                jnp.where(lane == by_token[:, k : k + 1], dense, 0.0), axis=1, keepdims=True
+            )
+            picked = picked + jnp.where(lane == k, value, 0.0)
+        combine_grad[...] = picked.T[: ids.shape[0]]
         inner = jnp.sum(gates[...] * dense, axis=1, keepdims=True)
         prob_grad = jnp.where(place[...] >= 0, (dense - inner) / scale[...], 0.0)
-        top = combine_grad.shape[1]
+        top = ids.shape[0]
         fraction = dense.shape[1] * counts[...] / (top * tokens * RING * RING)
         prob_grad = prob_grad + aux[0] * fraction
         mean = jnp.sum(probs[...] * prob_grad, axis=1, keepdims=True)
@@ -787,53 +832,63 @@
 
     order = (2, 1, -1, 0)
     work = [(k, p) for k in range(4) for p in range(3)]
-    values_line()
-    between = {2: values_x, 4: values_z, 6: router_back, 8: chip_sum}
-    for turn in range(len(work) + 1):
-        if turn < len(work):
-            k, p = work[turn]
-            if turn + 1 < len(work):
-                after_k, after_p = work[turn + 1]
-                for copy in given_copies(after_p, after_k, order[after_k]):
-                    copy.start()
-            produce(p, k, order[k])
-        if turn > 0:
-            k, p = work[turn - 1]
-            stage_copy(p, k, order[k]).wait()
-            give(p, k, order[k])
-            if p == 2 and k > 0:
-                for q in range(3):
-                    forward(q, k - 1, order[k - 1])
-        if turn in between:
-            between[turn]()
-        if turn == 8:
-            sum_send(0)
-    for p, (a, b, s) in enumerate(ORDERS):
-        gathered(p, 0, 2)
-        add_up(p, 2)
-        far = here.along(b, 2)
-        for k, step in enumerate(order):
-            for way, groups in ((1, pl.ds(0, 4)), (-1, pl.ds(4, 4))):
-                wires.send(
-                    rows[p].at[far, here.along(a, step), groups],
-                    halves2[p].at[0 if way == 1 else 1, k],
-                    here.near(b, way),
-                    (p, "half2", way, k),
-                )
-    for q in range(3):
-        forward(q, 3, order[3])
-    for k in (1, 2, 3):
+
+    def make(turn):
+        k, p = work[turn]
+        if turn + 1 < len(work):
+            after_k, after_p = work[turn + 1]
+            for copy in given_copies(after_p, after_k, order[after_k]):
+                copy.start()
+        produce(p, k, order[k])
+
+    def post(turn):
+        k, p = work[turn]
+        stage_copy(p, k, order[k]).wait()
+        give(p, k, order[k])
+
+    def pass_on(k):
+        for p in range(3):
+            forward(p, k, order[k])
+
+    def total(k):
         for p in range(3):
             gathered(p, k, order[k])
             add_up(p, order[k])
-    sum_in(0)
-    sum_send(1)
-    for k, step in enumerate(order):
-        for way in (1, -1):
+
+    def halve():
+        for p, (a, b, s) in enumerate(ORDERS):
+            far = here.along(b, 2)
+            for k, step in enumerate(order):
+                for way, groups in ((1, pl.ds(0, 4)), (-1, pl.ds(4, 4))):
+                    wires.send(
+                        rows[p].at[far, here.along(a, step), groups],
+                        halves2[p].at[0 if way == 1 else 1, k],
+                        here.near(b, way),
+                        (p, "half2", way, k),
+                    )
+
+    def fold(way):
+        for k, step in enumerate(order):
             for p in range(3):
                 fold2(p, way, k, step)
-    sum_in(1)
-    sum_send(2)
+
+    actions = {
+        "make": make,
+        "post": post,
+        "pass": pass_on,
+        "total": total,
+        "halve": halve,
+        "fold": fold,
+        "line": values_line,
+        "x": values_x,
+        "z": values_z,
+        "router": router_back,
+        "chip": chip_sum,
+        "send": sum_send,
+        "in": sum_in,
+    }
+    for name, *given_to in COMBINE_PLAN:
+        actions[name](*given_to)
     for p, (a, b, s) in enumerate(ORDERS):
         block = rows[p].at[here.at[b], here.along(a, 2)]
         block[...] = settle2(p, 0, 2).astype(jnp.bfloat16)
@@ -868,14 +923,15 @@
             preferred_element_type=jnp.float32,
         )
         out[:, pl.ds(start, size)] = total.astype(out.dtype)
-    sum_in(2)
+    if ("in", 2) not in COMBINE_PLAN:
+        sum_in(2)
     sum_out()
     wires.drain()
 
 
 def combine(parts, values, grads, weights, lines, counts, inputs, router, probs, gates, place, scale, ids, aux):
     width, units = weights[0].shape
-    tokens, top = ids.shape
+    top, tokens = ids.shape
     experts = probs.shape[1]
 
     def buffers(*lead):
@@ -890,7 +946,7 @@
         functools.partial(combine_kernel, parts),
         out_shape=(
             jax.ShapeDtypeStruct((tokens, width), jnp.bfloat16),
-            jax.ShapeDtypeStruct((tokens, top), jnp.float32),
+            jax.ShapeDtypeStruct((top, tokens), jnp.float32),
             jax.ShapeDtypeStruct((width // (2 * RING**3), experts), jnp.float32),
             jax.ShapeDtypeStruct((RING, RING, RING, 2, 16, width), jnp.bfloat16),
         ),
@@ -959,7 +1015,7 @@
     aux_weight,
 ):
     devices = lax.axis_size(AXES)
-    inputs, upstream_grad, chosen_ids = tokens[0], out_grad[0], expert_ids[0]
+    inputs, upstream_grad, chosen_ids = tokens[0], out_grad[0], expert_ids[0].T
     model_width = inputs.shape[1]
     capacity = saved_gate.shape[1] // devices
     parts = column_parts(model_width)
@@ -990,7 +1046,7 @@
         chosen_ids,
         aux_weight,
     )
-    return (token_grad[None], combine_grad[None], router_grad)
+    return (token_grad[None], combine_grad.T[None], router_grad)
 
 
 def solution(mesh):

time: 338 us -> 321 us (0.950)
  Pallas kernels: 314 us -> 299 us
    pallas_call x1, Pallas kernels: 168 us -> 155 us  [combine(): pl.pallas_call(functools.partial(combine_kernel, parts), out_shape=(jax.S...]
where the time goes in v3:
time: 321 us; the launch traced here: 316 us
  Pallas kernels  299 us (93%)
  other arithmetic  10.7 us (3%)
  local copies, waits for them, and re-layouts  4.93 us (2%)
    pallas_call x1, Pallas kernels, combine(): pl.pallas_call(functools.partial(combine_kernel, parts), out_shape=(jax.S...  155 us
    pallas_call x1, Pallas kernels, dispatch(): pl.pallas_call(functools.partial(dispatch_kernel, parts), out_shape=(jax....  145 us
    convert_element_type x1, other arithmetic, hidden_backward(): (upstream * second * gate_sig * (1.0 + first * (1.0 - gate_sig))).astype(...  9.94 us

profile of v3, /device:TPU:82, one launch (start us, length us, event | category | flops | bytes accessed | tf_op | source)
XLA Modules:
  0.0 316.1 jit_solution(9085912228281894393)
XLA Ops:
  1.3 144.6 %shard_map.121 = (bf16[4,4,4,2,16,4096]{5,4,3,2,1,0:T(8,128)(2,1)}, f32[4,4,4,2,16,768]{5,4,3,2,1,0:T(8,128)}, f32[3,4,4,8,128]{4,3,2,1,0:T(8,128)}, f32[1,128]{...) custom-call(bf16[128,4096]{1,0:T(8,128)(2,1)} %bitcast.26, ...), custom_call_target="tpu_custom_call" | custom-call | tf_op jit(solution)/shard_map/pallas_call | solution.py:459
  145.9 9.9 %fusion.4 = (bf16[4,4,4,2,16,768]{5,4,3,2,1,0:T(8,128)(2,1)}, bf16[4,4,4,2,16]{4,3,2,1,0:T(2,128)(2,1)S(1)}, bf16[4,4,4,2,16,768]{5,4,3,2,1,0:T(8,128)(2,1)}) fusion(f32[4,4,4,2,16,768]{5,4,3,2,1,0:T(8,128)} %get-tuple-element.13, bf16[4,4,4,2,16,768]{5,4,3,2,1,0:T(8,128)(2,1)} %bitcast.24, bf16[4,4,4,2,16,768]{5,4,3,2,1,0:T(8,128)(2,1)} %bitcast.25), kind=kLoop, calls=%fused_computation.9 | loop fusion | flops 28309504 | bytes 18878464 | tf_op jit(solution)/shard_map/convert_element_type | solution.py:998
  155.8 0.1 copy.13
  155.9 0.7 pad_convert_fusion.values
  156.6 154.6 %shard_map.122 = (bf16[128,4096]{1,0:T(8,128)(2,1)}, f32[8,128]{1,0:T(8,128)}, f32[32,128]{1,0:T(8,128)}, bf16[4,4,4,2,16,4096]{5,4,3,2,1,0:T(8,128)(2,1)}) custom-call(f32[4,4,4,2,1,128]{5,4,3,2,1,0:T(1,128)} %pad_convert_fusion.values, bf16[4,4,4,2,16,768]{5,4,3,2,1,0:T(8,128)(2,1)} %get-tuple-element.23.grad_first, ...), custom_call_target="tpu_custom_call" | custom-call | tf_op jit(solution)/shard_map/pallas_call | solution.py:945
  311.2 2.3 copy.18
  313.5 1.3 copy.19
  314.7 1.3 copy.20

commit v4 on v3

--- a/solution.py
+++ b/solution.py
@@ -109,10 +109,10 @@
 
 
 def dispatch_kernel(
-    parts, grad, inputs, router, ids, down,
-    slots, upstream, lines, counts, probs, gates, place, scale,
+    parts, grad, inputs, router, ids, down, saved_gate, saved_up,
+    slots, grad_first, grad_second, values, lines, counts, probs, gates, place, scale,
     g0, g1, g2, o0, o1, o2, l0, l1, l2, seen, picks, tokens_in, router_in, weight, batch, last,
-    ss, rs, ls, bs,
+    upstream, before, after, ss, rs, ls, bs, hs,
 ):
     held, outgoing, relay = (g0, g1, g2), (o0, o1, o2), (l0, l1, l2)
     here = Place()
@@ -133,11 +133,11 @@
         pltpu.make_async_copy(src, dst, bs.at[8 + n])
         for n, (src, dst) in enumerate(((inputs, tokens_in), (router, router_in), (down, weight)))
     ]
-    for copy in fetches:
-        copy.start()
     here.greet()
     for copy in local:
         copy.wait()
+    for copy in fetches[:2]:
+        copy.start()
 
     def pass_on(p, k, step):
         a, b, s = ORDERS[p]
@@ -201,6 +201,7 @@
             wires.send(block, block, here.near(a, way), (p, "m1", way))
     for copy in fetches[:2]:
         copy.wait()
+    fetches[2].start()
     route()
     for p, (a, b, s) in enumerate(ORDERS):
         table = seen.at[p, here.at[b], here.at[a]]
@@ -421,6 +422,74 @@
         counts[...] = jnp.sum(total, axis=0, keepdims=True)
         upstream[...] = jnp.zeros_like(upstream)
         fetches[2].wait()
+        for n in range(2):
+            for copy in saved_copies(n):
+                copy.start()
+
+    def saved_copies(n):
+        return [
+            pltpu.make_async_copy(
+                src.at[n // RING, n % RING], before.at[n % 2, i], hs.at[2 * (n % 2) + i]
+            )
+            for i, src in enumerate((saved_gate, saved_up))
+        ]
+
+    def grad_copies(n):
+        return [
+            pltpu.make_async_copy(
+                after.at[n % 2, i], dst.at[n // RING, n % RING], hs.at[4 + 2 * (n % 2) + i]
+            )
+            for i, dst in enumerate((grad_first, grad_second))
+        ]
+
+    def units_back():
+        rows = RING * RING
+
+        def one_block(n, carry):
+            z, x, slot = n // RING, n % RING, n % 2
+            for copy in saved_copies(n):
+                copy.wait()
+
+            @pl.when(n >= 2)
+            def _():
+                for copy in grad_copies(n):
+                    copy.wait()
+
+            def one_source(m, carry):
+                y, core = m // 2, m % 2
+                up = upstream[z, x, y, core]
+                first = before[slot, 0, y, core].astype(jnp.float32)
+                second = before[slot, 1, y, core].astype(jnp.float32)
+                sig = jax.nn.sigmoid(first)
+                act = first * sig
+                total = jnp.sum(up * (act * second), axis=-1, keepdims=True)
+                total = total.astype(jnp.bfloat16).astype(jnp.float32)
+                row = lax.broadcasted_iota(jnp.int32, (16, LANES), 0)
+                lane = lax.broadcasted_iota(jnp.int32, (16, LANES), 1)
+                values[z, x, y, core] = jnp.sum(
+                    jnp.where(row == lane, total, 0.0), axis=0, keepdims=True
+                )
+                after[slot, 0, y, core] = (
+                    up * second * sig * (1.0 + first * (1.0 - sig))
+                ).astype(jnp.bfloat16)
+                after[slot, 1, y, core] = (up * act).astype(jnp.bfloat16)
+                return carry
+
+            lax.fori_loop(0, 2 * RING, one_source, 0, unroll=8)
+            for copy in grad_copies(n):
+                copy.start()
+
+            @pl.when(n + 2 < rows)
+            def _():
+                for copy in saved_copies(n + 2):
+                    copy.start()
+
+            return carry
+
+        lax.fori_loop(0, rows, one_block, 0)
+        for n in (rows - 2, rows - 1):
+            for copy in grad_copies(n):
+                copy.wait()
 
     def multiply(k, arrive, senders):
         def fetch(p):
@@ -445,10 +514,11 @@
     }
     for name, *given_to in DISPATCH_PLAN:
         actions[name](*given_to)
+    units_back()
     wires.drain()
 
 
-def dispatch(parts, grad, inputs, router, ids, down):
+def dispatch(parts, grad, inputs, router, ids, down, saved_gate, saved_up):
     tokens, width = grad.shape
     units, experts = down.shape[0], router.shape[1]
     rows = [pltpu.VMEM((RING, RING, tokens, size), jnp.bfloat16) for _, size in parts]
@@ -460,7 +530,9 @@
         functools.partial(dispatch_kernel, parts),
         out_shape=(
             jax.ShapeDtypeStruct((RING, RING, RING, 2, 16, width), jnp.bfloat16),
-            jax.ShapeDtypeStruct((RING, RING, RING, 2, 16, units), jnp.float32),
+            jax.ShapeDtypeStruct((RING, RING, RING, 2, 16, units), jnp.bfloat16),
+            jax.ShapeDtypeStruct((RING, RING, RING, 2, 16, units), jnp.bfloat16),
+            jax.ShapeDtypeStruct((RING, RING, RING, 2, 1, LANES), jnp.float32),
             jax.ShapeDtypeStruct((3, RING, RING, 8, LANES), jnp.float32),
             jax.ShapeDtypeStruct((1, experts), jnp.float32),
             square,
@@ -468,8 +540,8 @@
             square,
             jax.ShapeDtypeStruct((tokens, 1), jnp.float32),
         ),
-        in_specs=[hbm, hbm, hbm, vmem, hbm],
-        out_specs=(hbm,) + (vmem,) * 7,
+        in_specs=[hbm, hbm, hbm, vmem, hbm, hbm, hbm],
+        out_specs=(hbm,) * 3 + (vmem,) * 7,
         scratch_shapes=rows
         + outs
         + relays
@@ -481,15 +553,19 @@
             pltpu.VMEM((units, width), jnp.bfloat16),
             pltpu.VMEM((2, 3, RING, 2, 16, parts[0][1]), jnp.bfloat16),
             pltpu.VMEM((2, 1, RING, 2, 16, parts[0][1]), jnp.bfloat16),
+            pltpu.VMEM((RING, RING, RING, 2, 16, units), jnp.float32),
+            pltpu.VMEM((2, 2, RING, 2, 16, units), jnp.bfloat16),
+            pltpu.VMEM((2, 2, RING, 2, 16, units), jnp.bfloat16),
             pltpu.SemaphoreType.DMA((192,)),
             pltpu.SemaphoreType.DMA((192,)),
             pltpu.SemaphoreType.DMA((32,)),
             pltpu.SemaphoreType.DMA((11,)),
+            pltpu.SemaphoreType.DMA((8,)),
         ],
         compiler_params=pltpu.CompilerParams(
             collective_id=0, has_side_effects=True, vmem_limit_bytes=62 * 2**20
         ),
-    )(grad, inputs, router, ids, down)[1:]
+    )(grad, inputs, router, ids, down, saved_gate, saved_up)[1:]
 
 
 def combine_kernel(
@@ -515,8 +591,9 @@
         for n, (src, dst) in enumerate(((w_gate, gate), (w_up, up))):
             span = pl.ds(start, size)
             copy = pltpu.make_async_copy(src.at[span], dst.at[span], bs.at[6 + 2 * p + n])
-            copy.start()
             fetches.append(copy)
+    for copy in fetches[:2]:
+        copy.start()
 
     def given_copies(p, k, b_step):
         slot = (k * 3 + p) % 2
@@ -529,6 +606,8 @@
     for copy in given_copies(0, 0, 2):
         copy.start()
     here.greet(steps)
+    for copy in fetches[2:]:
+        copy.start()
 
     def values_line():
         mine = here.at[2] * 2 + here.core
@@ -988,20 +1067,6 @@
     )(values, *grads, *weights, lines, counts, inputs, router, probs, gates, place, scale, ids, aux)[:3]
 
 
-def hidden_backward(upstream, pre_gate, pre_up):
-    first = pre_gate.astype(jnp.float32)
-    second = pre_up.astype(jnp.float32)
-    gate_sig = jax.nn.sigmoid(first)
-    gate_act = first * gate_sig
-    hidden = gate_act * second
-    slot_combine = jnp.sum(upstream * hidden, axis=-1).astype(jnp.bfloat16)
-    grad_first = (upstream * second * gate_sig * (1.0 + first * (1.0 - gate_sig))).astype(
-        jnp.bfloat16
-    )
-    grad_second = (upstream * gate_act).astype(jnp.bfloat16)
-    return grad_first, grad_second, slot_combine
-
-
 def shards(
     tokens,
     out_grad,
@@ -1017,19 +1082,19 @@
     devices = lax.axis_size(AXES)
     inputs, upstream_grad, chosen_ids = tokens[0], out_grad[0], expert_ids[0].T
     model_width = inputs.shape[1]
-    capacity = saved_gate.shape[1] // devices
     parts = column_parts(model_width)
 
-    upstream, lines, counts, probs, gates, place, chosen_sum = dispatch(
-        parts, upstream_grad, inputs, router_weight, chosen_ids, down_weight[0]
+    by_source = (RING, RING, RING, 2, saved_gate.shape[1] // devices, saved_gate.shape[2])
+    grad_first, grad_second, values, lines, counts, probs, gates, place, chosen_sum = dispatch(
+        parts,
+        upstream_grad,
+        inputs,
+        router_weight,
+        chosen_ids,
+        down_weight[0],
+        saved_gate[0].reshape(by_source),
+        saved_up[0].reshape(by_source),
     )
-    grad_first, grad_second, slot_combine = hidden_backward(
-        upstream,
-        saved_gate[0].reshape(upstream.shape),
-        saved_up[0].reshape(upstream.shape),
-    )
-    values = slot_combine.astype(jnp.float32).reshape(*upstream.shape[:4], 1, capacity)
-    values = jnp.pad(values, [(0, 0)] * 5 + [(0, LANES - capacity)])
     token_grad, combine_grad, router_grad = combine(
         parts,
         values,

time: 321 us -> 319 us (level)
  other arithmetic: 10.7 us -> 0 us
  Pallas kernels: 299 us -> 309 us
    convert_element_type x1 -> x0, other arithmetic: 9.94 us -> none  [hidden_backward(): (upstream * second * gate_sig * (1.0 + first * (1.0 - gate_sig))).astype(...]
    pallas_call x1, Pallas kernels: 145 us -> 154 us  [dispatch(): pl.pallas_call(functools.partial(dispatch_kernel, parts), out_shape=(jax....]
where the time goes in v4:
time: 319 us; the launch traced here: 315 us
  Pallas kernels  309 us (97%)
  local copies, waits for them, and re-layouts  4.88 us (2%)
    pallas_call x1, Pallas kernels, combine(): pl.pallas_call(functools.partial(combine_kernel, parts), out_shape=(jax.S...  155 us
    pallas_call x1, Pallas kernels, dispatch(): pl.pallas_call(functools.partial(dispatch_kernel, parts), out_shape=(jax....  154 us

profile of v4, /device:TPU:82, one launch (start us, length us, event | category | flops | bytes accessed | tf_op | source)
XLA Modules:
  0.0 314.9 jit_solution(422193871789305414)
XLA Ops:
  1.3 153.8 %shard_map.121 = (bf16[4,4,4,2,16,4096]{5,4,3,2,1,0:T(8,128)(2,1)}, bf16[4,4,4,2,16,768]{5,4,3,2,1,0:T(8,128)(2,1)}, bf16[4,4,4,2,16,768]{5,4,3,2,1,0:T(8,128)(2...) custom-call(bf16[128,4096]{1,0:T(8,128)(2,1)} %bitcast.21, ...), custom_call_target="tpu_custom_call" | custom-call | tf_op jit(solution)/shard_map/pallas_call | solution.py:529
  155.1 154.9 %shard_map.122 = (bf16[128,4096]{1,0:T(8,128)(2,1)}, f32[8,128]{1,0:T(8,128)}, f32[32,128]{1,0:T(8,128)}, bf16[4,4,4,2,16,4096]{5,4,3,2,1,0:T(8,128)(2,1)}) custom-call(f32[4,4,4,2,1,128]{5,4,3,2,1,0:T(1,128)} %get-tuple-element.15.values, bf16[4,4,4,2,16,768]{5,4,3,2,1,0:T(8,128)(2,1)} %get-tuple-element.16.grad_first, ...), custom_call_target="tpu_custom_call" | custom-call | tf_op jit(solution)/shard_map/pallas_call | solution.py:1024
  310.0 2.3 copy.17
  312.3 1.3 copy.18
  313.6 1.3 copy.19
